TPU v7x, 256 devices: a whole 4x4x8 slice. The times are simulated.
256 devices in a mesh: gx: 8 (over x, z_lo), gy: 8 (over z_hi, core), ha: 4 (over y).
Axes of the slice: x: 4, y: 4, z: 8 (z_hi: 4, z_lo: 2; z = z_hi * 2 + z_lo), core: 2. Of those that a mesh axis runs over, the one named last changes fastest.
Arguments:
- density: bfloat16 [3, 625, 8, 8, 1024], P(None, None, 'gx', 'gy', 'ha'), may hold values from -6 to 6
- upsample: bfloat16 [2112, 625], replicated, may hold values from -0.25 to 0.25
- normal_kernel: bfloat16 [625, 2112], replicated, may hold values from -0.125 to 0.125
- tangent_kernel: bfloat16 [625, 2112], replicated, may hold values from -0.125 to 0.125
- self_operator: bfloat16 [625, 625], replicated, may hold values from -0.25 to 0.25
- rim_list: int32 [8, 8, 128], P('gx', 'gy', 'ha'), may hold values from 0 to 255
- pair_target: int32 [8, 8, 4, 256], P('gx', 'gy', 'ha'), may hold values from 0 to 1023
- pair_source: int32 [8, 8, 4, 256], P('gx', 'gy', 'ha'), may hold values from 0 to 2175
- pair_weight: float32 [8, 8, 4, 256], P('gx', 'gy', 'ha'), may hold values from 0.5 to 2
- pair_angles: float32 [3, 8, 8, 4, 256], P(None, 'gx', 'gy', 'ha'), may hold values from -3.140625 to 3.140625
- live_count: int32 [8, 8, 4], P('gx', 'gy', 'ha'), may hold values from 1 to 256, as said below
Outputs:
- induced: float32 [3, 625, 8, 8, 1024], P(None, None, 'gx', 'gy', 'ha')
Inputs may be any that keep to these rules, and one draw needn't show every extreme that they name: `rim_list`: an index into the device's own 256 grains. `pair_target`: an index into the 1024 grains of the pair's slab. `pair_source`: an index into the slab's source pool. `live_count`: some device uses all 256 slots.
All inputs are finite; a program needn't handle non-finite values.
Results may differ from a plain program's by a relative error of at most 0.0024.
Values may be sent and summed in bfloat16 or wider, within the bound.
A program may use at most 128 MiB of HBM per device.

v0:
```python
import jax
import jax.numpy as jnp
from jax import lax
from jax.sharding import PartitionSpec as P


def with_halo(cells, sides, width):
    for axis, dim in sides:
        count = lax.axis_size(axis)
        head = lax.slice_in_dim(cells, 0, width, axis=dim)
        tail = lax.slice_in_dim(cells, cells.shape[dim] - width, cells.shape[dim], axis=dim)
        cells = jnp.concatenate(
            [
                lax.ppermute(tail, axis, [(i, (i + 1) % count) for i in range(count)]),
                cells,
                lax.ppermute(head, axis, [((i + 1) % count, i) for i in range(count)]),
            ],
            axis=dim,
        )
    return cells


def rotation(angles):
    first, second, third = (angles[0], angles[1], angles[2])
    all_zeros = jnp.zeros_like(first)
    all_ones = jnp.ones_like(first)

    def about_z(angle_value):
        cosine, sine_value = (jnp.cos(angle_value), jnp.sin(angle_value))
        return jnp.stack(
            [
                jnp.stack([cosine, -sine_value, all_zeros]),
                jnp.stack([sine_value, cosine, all_zeros]),
                jnp.stack([all_zeros, all_zeros, all_ones]),
            ]
        )

    cosine, sine_value = (jnp.cos(second), jnp.sin(second))
    tilt = jnp.stack(
        [
            jnp.stack([cosine, all_zeros, sine_value]),
            jnp.stack([all_zeros, all_ones, all_zeros]),
            jnp.stack([-sine_value, all_zeros, cosine]),
        ]
    )
    return jnp.einsum(
        "abp,bcp,cdp->adp", about_z(first), tilt, about_z(third), precision=lax.Precision.HIGHEST
    )


def spread(own_data, rim_data):
    slab_data, slab_rims = (
        lax.all_gather(own_data, "ha", axis=2, tiled=True),
        lax.all_gather(rim_data, "ha", axis=2, tiled=True),
    )
    lifted = slab_rims[:, :, None, None, :]
    beside_all = with_halo(lifted, (("gx", 2), ("gy", 3)), 1)
    return (slab_data, beside_all)


def evaluate(upsample, coefficients):
    return jnp.einsum(
        "qk,ckg->cqg", upsample, coefficients, preferred_element_type=jnp.float32
    ).astype(jnp.bfloat16)


def shards(
    density,
    upsample,
    normal_kernel,
    tangent_kernel,
    self_operator,
    rim_list,
    pair_target,
    pair_source,
    pair_weight,
    pair_angles,
    live_count,
):
    width = density.shape[1]
    grain_count = density.shape[4]
    owned = density.reshape(3, width, grain_count)
    rim_index = rim_list.reshape(-1)
    slab_data, beside_all = spread(owned, jnp.take(owned, rim_index, axis=2))
    source_pool = jnp.concatenate(
        [slab_data, beside_all.reshape(3, slab_data.shape[1], -1)], axis=2
    )
    source = pair_source.reshape(-1)
    target = pair_target.reshape(-1)
    picked = jnp.take(source_pool, source, axis=2)
    node_values = evaluate(upsample, picked)
    slot_total = source.shape[0]
    alive_mask = jnp.arange(slot_total, dtype=jnp.int32) < live_count.reshape(())
    scaling = jnp.where(alive_mask, pair_weight.reshape(-1), jnp.float32(0.0))
    frames = rotation(pair_angles.reshape(3, slot_total))
    rotated = (
        frames[:, 0, None, :] * node_values[0]
        + frames[:, 1, None, :] * node_values[1]
        + frames[:, 2, None, :] * node_values[2]
    ).astype(jnp.bfloat16)
    quad_normal = jnp.dot(normal_kernel, rotated[0], preferred_element_type=jnp.float32)
    quad_tangent = jnp.einsum(
        "kq,cqp->ckp", tangent_kernel, rotated[1:], preferred_element_type=jnp.float32
    )
    quad = jnp.concatenate([quad_normal[None], quad_tangent], axis=0)
    contribution = (
        frames[0, :, None, :] * quad[0]
        + frames[1, :, None, :] * quad[1]
        + frames[2, :, None, :] * quad[2]
    ) * scaling[None, None, :]
    slab_total = grain_count * lax.axis_size("ha")
    partial_value = (
        jnp.zeros((3, width, slab_total), jnp.float32).at[:, :, target].add(contribution)
    )
    summed = lax.psum_scatter(partial_value, "ha", scatter_dimension=2, tiled=True)
    self_term = jnp.einsum("jk,ckg->cjg", self_operator, owned, preferred_element_type=jnp.float32)
    return (summed + self_term).reshape(3, width, 1, 1, grain_count)


def solution(mesh):
    return jax.shard_map(
        shards,
        mesh=mesh,
        in_specs=(
            P(None, None, "gx", "gy", "ha"),
            P(),
            P(),
            P(),
            P(),
            P("gx", "gy", "ha"),
            P("gx", "gy", "ha", None),
            P("gx", "gy", "ha", None),
            P("gx", "gy", "ha", None),
            P(None, "gx", "gy", "ha", None),
            P("gx", "gy", "ha"),
        ),
        out_specs=P(None, None, "gx", "gy", "ha"),
        check_vma=False,
    )
```

profile of v0, /device:TPU:1, one launch (start us, length us, event | category | flops | bytes accessed | tf_op | source)
XLA Modules:
  0.0 314.5 jit_solution(326171155795648703)
XLA Ops:
  6.5 0.7 all-gather.3.cloned.1.call-update
  7.3 3.4 %copy.58 = bf16[3,625,1,1,256]{1,0,4,3,2:T(4,128)(2,1)} copy(bf16[3,625,1,1,256]{4,1,3,2,0:T(8,128)(2,1)} %param.11) | data formatting | bytes 1920000 | tf_op args[0]
  10.8 2.0 gather_fusion
  13.0 12.5 %all_gather.7 = bf16[3,625,128]{1,2,0:T(8,128)(2,1)S(1)} all-gather(bf16[3,625,32]{1,2,0:T(8,128)(2,1)S(1)} %copy.59), channel_id=1, replica_groups=mesh['gx'=8,'gy'=8,'ha'=4] {'ha'}, dimensions={2}, use_global_device_ids=true | all-gather | bytes 600000 | tf_op jit(solution)/shard_map/all_gather | solution.py:54
  25.5 1.0 copy.60
  26.5 3.8 %collective-permute-start.1 = (bf16[3,625,1,1,128]{4,1,3,2,0:T(8,128)(2,1)}, bf16[3,625,1,1,128]{4,1,3,2,0:T(8,128)(2,1)}, u32[]{:S(2)}, u32[]{:S(2)}) collective-permute-start(bf16[3,625,1,1,128]{4,1,3,2,0:T(8,128)(2,1)} %copy.60), channel_id=1, source_target_pairs={{32,0},{64,32},{96,64},{128,96},{160,128},{192,160},{224,192},{0,2... | collective-permute-start | bytes 1440008 | tf_op jit(solution)/shard_map/ppermute | solution.py:16
  31.3 1.0 copy.55
  32.4 1.0 copy.53
  33.4 1.0 copy.52
  34.4 3.0 convolution_bitcast_fusion.2
  37.4 3.2 %convolution_bitcast_fusion.1 = f32[3,3,256]{1,0,2:T(4,128)S(1)} fusion(f32[3,256,3]{2,0,1:T(4,128)S(1)} %convolution_bitcast_fusion.2, f32[3,3,256]{1,0,2:T(4,128)} %copy.55), kind=kOutput, calls=%fused_computation.18 | convolution fusion | flops 82944 | bytes 27648 | tf_op jit(solution)/shard_map/abp,bcp,cdp->adp/dot_general | solution.py:46
  40.7 2.0 copy.63
  42.7 7.5 %collective-permute-done = bf16[3,625,1,1,128]{4,1,3,2,0:T(8,128)(2,1)} collective-permute-done((bf16[3,625,1,1,128]{4,1,3,2,0:T(8,128)(2,1)}, bf16[3,625,1,1,128]{4,1,3,2,0:T(8,128)(2,1)}, u32[]{:S(2)}, u32[]{:S(2)}) %collective-permute-start) | collective-permute-done | bytes 480032 | tf_op jit(solution)/shard_map/ppermute | solution.py:14
  50.2 2.0 copy.62
  52.3 2.7 pad_maximum_fusion.2
  55.0 3.6 %copy.64 = bf16[3,625,3,1,128]{4,1,3,2,0:T(8,128)(2,1)} copy(bf16[3,625,3,1,128]{1,4,0,3,2:T(8,128)(2,1)} %pad_maximum_fusion.2) | data formatting | bytes 2880000 | tf_op jit(solution)/shard_map/concatenate | solution.py:12
  58.6 3.0 collective-permute-start.3
  61.6 3.1 collective-permute-start.2
  64.7 1.8 fusion.27
  66.5 1.2 copy.56
  67.7 1.2 copy.72
  69.0 1.2 copy.71
  70.3 1.0 fusion.26
  71.3 26.1 %collective-permute-done.3 = bf16[3,625,3,1,128]{4,1,3,2,0:T(8,128)(2,1)} collective-permute-done((bf16[3,625,3,1,128]{4,1,3,2,0:T(8,128)(2,1)}, bf16[3,625,3,1,128]{4,1,3,2,0:T(8,128)(2,1)}, u32[]{:S(2)}, u32[]{:S(2)}) %collective-permute-start.3) | collective-permute-done | bytes 1440032 | tf_op jit(solution)/shard_map/ppermute | solution.py:16
  97.3 3.6 %copy.67 = bf16[3,625,3,1,128]{1,4,0,3,2:T(8,128)(2,1)} copy(bf16[3,625,3,1,128]{4,1,3,2,0:T(8,128)(2,1)} %collective-permute-done.3) | data formatting | bytes 2880000 | tf_op jit(solution)/shard_map/ppermute | solution.py:16
  100.9 3.6 %copy.66 = bf16[3,625,3,1,128]{1,4,0,3,2:T(8,128)(2,1)} copy(bf16[3,625,3,1,128]{4,1,3,2,0:T(8,128)(2,1)} %collective-permute-done.2) | data formatting | bytes 2880000 | tf_op jit(solution)/shard_map/ppermute | solution.py:14
  104.6 2.6 pad_maximum_fusion.1
  107.1 0.7 copy.68
  107.8 18.2 %copy.69 = bf16[3,625,1152]{1,0,2:T(4,128)(2,1)} copy(bf16[3,625,1152]{1,2,0:T(8,128)(2,1)S(1)} %bitcast.118) | data formatting | bytes 8640000 | tf_op jit(solution)/shard_map/reshape | solution.py:86
  126.0 8.8 %copy.57 = bf16[3,625,1,1,1024]{1,0,4,3,2:T(4,128)(2,1)} copy(bf16[3,625,1,1,1024]{4,1,3,2,0:T(8,128)(2,1)} %all-gather.3.cloned.1.call-done) | data formatting | bytes 7680000 | tf_op jit(solution)/shard_map/all_gather | solution.py:53
  134.8 17.9 %pad_maximum_fusion = bf16[3,625,2176]{1,0,2:T(4,128)(2,1)} fusion(bf16[3,625,1152]{1,0,2:T(4,128)(2,1)} %copy.69, bf16[3,625,1024]{1,0,2:T(4,128)(2,1)} %bitcast.117), kind=kLoop, calls=%fused_computation.3 | loop fusion | flops 4080000 | bytes 16320000 | tf_op jit(solution)/shard_map/concatenate | solution.py:85
  152.8 7.0 %gather_fusion.1 = bf16[256,3,625]{2,1,0:T(4,128)(2,1)} fusion(bf16[3,625,2176]{1,0,2:T(4,128)(2,1)} %pad_maximum_fusion, s32[1024]{0:T(1024)S(1)} %pad_clamp_fusion), kind=kCustom, calls=%fused_computation.1 | custom fusion | bytes 1921024 | tf_op jit(solution)/shard_map/jit(_take)/gather | solution.py:90
  159.8 2.4 select_bitcast_fusion
  162.2 2.7 fusion
  164.9 0.4 fusion.10
  165.4 1.3 add_convert_fusion
  166.7 0.4 copy-done.11
  167.1 2.1 convolution_bitcast_fusion
  169.2 1.7 fusion.5
  171.3 2.2 copy.73
  173.5 1.1 copy.75
  174.5 3.3 %multiply_bitcast_fusion = f32[256,3,625]{2,1,0:T(4,128)S(1)} fusion(f32[256]{0:T(256)S(1)} %compare_select_fusion.5, f32[625,256]{0,1:T(8,128)} %copy.75, f32[3,256]{0,1:T(8,128)} %bitcast.125, f32[625,256]{0,1:T(8,128)S(1)} %copy.74, f32[3,256]{0,1:T(8,128)} %bitcast.126, f32[625,256]{0,1:T(8,128)} %copy.73, f32[3,256]{0,1:T(8,128)S(1)} %bitcast.124), kind=kLoop, calls=%fused_computation.11 | loop fusion | flops 2880000 | bytes 3850240 | tf_op jit(solution)/shard_map/mul | solution.py:106
  177.9 5.4 %broadcast_in_dim.36 = f32[3,625,1024]{1,0,2:T(4,128)} broadcast(f32[]{:T(128)} %constant.12.clone.1), dimensions={} | broadcast | bytes 7680004 | tf_op jit(solution)/shard_map/broadcast_in_dim | solution.py:113
  183.2 31.4 %scatter_fusion = f32[3,625,1024]{1,0,2:T(4,128)} fusion(f32[3,625,1024]{1,0,2:T(4,128)} %broadcast_in_dim.36, s32[256]{0:T(256)S(1)} %bitcast.130, f32[256,3,625]{2,1,0:T(4,128)S(1)} %multiply_bitcast_fusion), kind=kCustom, calls=%fused_computation.2 | custom fusion | flops 480000 | bytes 5761024 | tf_op jit(solution)/shard_map/scatter-add | solution.py:113
  214.6 11.2 %copy.76 = f32[3,625,1024]{2,1,0:T(8,128)} copy(f32[3,625,1024]{1,0,2:T(4,128)} %scatter_fusion) | data formatting | bytes 15360000 | tf_op jit(solution)/shard_map/scatter-add | solution.py:113
  225.9 75.5 %reduce-scatter.2.cloned.1.call-done = f32[3,625,256]{2,1,0:T(8,128)} async-done(((f32[3,625,1024]{2,1,0:T(8,128)}), f32[3,625,256]{2,1,0:T(8,128)}) %reduce-scatter.2.cloned.1.call-update) | async-done | bytes 1920016 | tf_op jit(solution)/shard_map/reduce_scatter | solution.py:115
  301.4 3.1 fusion.4
  304.4 3.2 %copy.78 = f32[3,625,1,1,256]{4,3,2,1,0:T(1,128)} copy(f32[3,625,1,1,256]{4,1,0,3,2:T(8,128)S(1)} %fusion.4) | data formatting | bytes 3840000 | tf_op jit(solution)/shard_map/reshape | solution.py:117
  (51 shorter events, 0.9 us)
Async XLA Ops:
  6.5 155.7 %copy-start = (bf16[2112,625]{1,0:T(8,128)(2,1)S(1)}, bf16[2112,625]{1,0:T(8,128)(2,1)}, u32[]{:S(2)}) copy-start(bf16[2112,625]{1,0:T(8,128)(2,1)} %param.12) | copy-start | bytes 7920004
  6.5 4.2 %copy-start.13 = (s32[1,1,32]{2,1,0:T(1,128)S(1)}, s32[1,1,32]{2,1,0:T(1,128)}, u32[]{:S(2)}) copy-start(s32[1,1,32]{2,1,0:T(1,128)} %param.16) | copy-start | bytes 388
  6.5 119.5 %all-gather.3.cloned.1.call-start = ((), (), s32[]{:S(2)}) async-start(), calls=%async_computation.2 | async-start | bytes 4853760 | tf_op jit(solution)/shard_map/all_gather | solution.py:53
  7.3 23.8 %copy-start.5 = (f32[3,1,1,1,256]{4,3,2,1,0:T(1,128)S(1)}, f32[3,1,1,1,256]{4,3,2,1,0:T(1,128)}, u32[]{:S(2)}) copy-start(f32[3,1,1,1,256]{4,3,2,1,0:T(1,128)} %param.20) | copy-start | bytes 9220
  7.3 24.0 %copy-start.6 = (f32[1,3,256]{2,1,0:T(4,128)S(1)}, f32[1,3,256]{2,1,0:T(4,128)}, u32[]{:S(2)}) copy-start(f32[1,3,256]{2,1,0:T(4,128)} %constant.22.clone.1) | copy-start | bytes 9220
  7.3 24.0 %copy-start.7 = (f32[1,3,256]{2,1,0:T(4,128)S(1)}, f32[1,3,256]{2,1,0:T(4,128)}, u32[]{:S(2)}) copy-start(f32[1,3,256]{2,1,0:T(4,128)} %constant.21.clone.1) | copy-start | bytes 9220
  7.3 294.1 %reduce-scatter.2.cloned.1.call-start = ((), (), s32[]{:S(2)}) async-start(), calls=%async_computation.1 | async-start | bytes 9707520 | tf_op jit(solution)/shard_map/reduce_scatter | solution.py:115
  25.5 8.9 %copy-start.2 = (bf16[3,625,128]{1,2,0:T(8,128)(2,1)}, bf16[3,625,128]{1,2,0:T(8,128)(2,1)S(1)}, u32[]{:S(2)}) copy-start(bf16[3,625,128]{1,2,0:T(8,128)(2,1)S(1)} %all_gather.7) | copy-start | bytes 1440004
  26.5 14.1 %collective-permute-start.1 = (bf16[3,625,1,1,128]{4,1,3,2,0:T(8,128)(2,1)}, bf16[3,625,1,1,128]{4,1,3,2,0:T(8,128)(2,1)}, u32[]{:S(2)}, u32[]{:S(2)}) collective-permute-start(bf16[3,625,1,1,128]{4,1,3,2,0:T(8,128)(2,1)} %copy.60), channel_id=1, source_target_pairs={{32,0},{64,32},{96,64},{128,96},{160,128},{192,160},{224,192},{0,2... | collective-permute-start | bytes 1440008 | tf_op jit(solution)/shard_map/ppermute | solution.py:16
  30.4 19.9 %collective-permute-start = (bf16[3,625,1,1,128]{4,1,3,2,0:T(8,128)(2,1)}, bf16[3,625,1,1,128]{4,1,3,2,0:T(8,128)(2,1)}, u32[]{:S(2)}, u32[]{:S(2)}) collective-permute-start(bf16[3,625,1,1,128]{4,1,3,2,0:T(8,128)(2,1)} %copy.60), channel_id=1, source_target_pairs={{0,32},{32,64},{64,96},{96,128},{128,160},{160,192},{192,224},{224... | collective-permute-start | bytes 1440008 | tf_op jit(solution)/shard_map/ppermute | solution.py:14
  58.6 11.6 %copy-start.8 = (s32[1,1,1,256]{3,2,1,0:T(1,128)S(1)}, s32[1,1,1,256]{3,2,1,0:T(1,128)}, u32[]{:S(2)}) copy-start(s32[1,1,1,256]{3,2,1,0:T(1,128)} %param.18) | copy-start | bytes 3076
  58.6 11.6 %copy-start.9 = (s32[1,1,1,256]{3,2,1,0:T(1,128)S(1)}, s32[1,1,1,256]{3,2,1,0:T(1,128)}, u32[]{:S(2)}) copy-start(s32[1,1,1,256]{3,2,1,0:T(1,128)} %param.17) | copy-start | bytes 3076
  58.6 11.6 %copy-start.10 = (f32[1,1,1,256]{3,2,1,0:T(1,128)S(1)}, f32[1,1,1,256]{3,2,1,0:T(1,128)}, u32[]{:S(2)}) copy-start(f32[1,1,1,256]{3,2,1,0:T(1,128)} %param.19) | copy-start | bytes 3076
  58.6 38.7 %collective-permute-start.3 = (bf16[3,625,3,1,128]{4,1,3,2,0:T(8,128)(2,1)}, bf16[3,625,3,1,128]{4,1,3,2,0:T(8,128)(2,1)}, u32[]{:S(2)}, u32[]{:S(2)}) collective-permute-start(bf16[3,625,3,1,128]{4,1,3,2,0:T(8,128)(2,1)} %copy.64), channel_id=1, source_target_pairs={{4,0},{8,4},{12,8},{16,12},{20,16},{24,20},{28,24},{0,28},{5,1},{9... | collective-permute-start | bytes 4320008 | tf_op jit(solution)/shard_map/ppermute | solution.py:16
  61.6 39.3 %collective-permute-start.2 = (bf16[3,625,3,1,128]{4,1,3,2,0:T(8,128)(2,1)}, bf16[3,625,3,1,128]{4,1,3,2,0:T(8,128)(2,1)}, u32[]{:S(2)}, u32[]{:S(2)}) collective-permute-start(bf16[3,625,3,1,128]{4,1,3,2,0:T(8,128)(2,1)} %copy.64), channel_id=1, source_target_pairs={{0,4},{4,8},{8,12},{12,16},{16,20},{20,24},{24,28},{28,0},{1,5},{5... | collective-permute-start | bytes 4320008 | tf_op jit(solution)/shard_map/ppermute | solution.py:14
  71.3 33.3 %copy-start.3 = (bf16[3,625,128]{1,2,0:T(8,128)(2,1)S(1)}, bf16[3,625,128]{1,2,0:T(8,128)(2,1)}, u32[]{:S(2)}) copy-start(bf16[3,625,128]{1,2,0:T(8,128)(2,1)} %copy-done.2) | copy-start | bytes 1440004
  165.4 1.8 copy-start.11
  167.1 2.1 copy-start.12
  225.9 75.5 %copy-start.4 = (bf16[625,625]{1,0:T(8,128)(2,1)S(1)}, bf16[625,625]{1,0:T(8,128)(2,1)}, u32[]{:S(2)}) copy-start(bf16[625,625]{1,0:T(8,128)(2,1)} %param.15) | copy-start | bytes 2343754
  301.4 6.3 %copy-start.1 = (bf16[2112,625]{1,0:T(8,128)(2,1)S(1)}, bf16[2112,625]{1,0:T(8,128)(2,1)}, u32[]{:S(2)}) copy-start(bf16[2112,625]{1,0:T(8,128)(2,1)} %param.12) | copy-start | bytes 7920004
Sparse Core Ops, SparseCore 0:
  9.1 53.7 all-gather.2
  226.0 75.3 reduce-scatter.1
where the time goes:
time: 317 us; the launch traced here: 315 us
  waiting for transfers between devices  110 us (35%)
  local copies, waits for them, and re-layouts  89.6 us (28%)
  other arithmetic  62.5 us (20%)
  matrix products  15.8 us (5%)
  between operations  14.4 us (5%)
  blocking collectives  12.5 us (4%)
  starting transfers between devices  9.99 us (3%)
    reduce_scatter x1, waiting for transfers between devices, shards(): lax.psum_scatter(partial_value, 'ha', scatter_dimension=2, tiled=True)  75.5 us
    scatter-add x1, other arithmetic, shards(): jnp.zeros((3, width, slab_total), jnp.float32).at[:, :, target]  31.4 us
    ppermute x2, waiting for transfers between devices, with_halo(): lax.ppermute(head, axis, [((i + 1) % count, i) for i in range(count)])  26.1 us
    reshape x1, local copies, waits for them, and re-layouts, shards(): beside_all.reshape(3, slab_data.shape[1], -1)  18.2 us
    concatenate x1, other arithmetic, shards(): jnp.concatenate([slab_data, beside_all.reshape(3, slab_data.shape[1], -1)...  17.9 us
    all_gather x1, blocking collectives, spread(): lax.all_gather(rim_data, 'ha', axis=2, tiled=True)  12.5 us
    scatter-add x1, local copies, waits for them, and re-layouts, shards(): jnp.zeros((3, width, slab_total), jnp.float32).at[:, :, target]  11.2 us
    all_gather x1, local copies, waits for them, and re-layouts, spread(): lax.all_gather(own_data, 'ha', axis=2, tiled=True)  8.79 us
  transfers between devices with their start and end apart: 6, of which 3 were waited for; matrix products, arithmetic and copies ran while one was open for 20% of the time, Pallas kernels for 0%

commit v1 on v0

v1 whole, which is shorter than its diff:
```python
import functools

import jax
import jax.numpy as jnp
from jax import lax
from jax.experimental import pallas as pl
from jax.experimental.pallas import tpu as pltpu
from jax.sharding import PartitionSpec as P

MESH = pl.DeviceIdType.MESH
ANY = pl.BlockSpec(memory_space=pl.ANY)
VMEM = pl.BlockSpec(memory_space=pltpu.VMEM)
SMEM = pl.BlockSpec(memory_space=pltpu.SMEM)
CAPACITY = 96
TABLE = 16
SCALE, SOURCE_PLACE, SOURCE_COLUMN, TARGET_PLACE, TARGET_COLUMN = 9, 10, 11, 12, 13
NT = (((1,), (1,)), ((), ()))
TN = (((0,), (0,)), ((), ()))
F32 = jnp.float32
BF16 = jnp.bfloat16


def padded(width):
    return (width + 127) // 128 * 128


def local_params():
    return pltpu.CompilerParams(vmem_limit_bytes=58 * 1024 * 1024)


def pair_table(angles, weight, source, target, live, grains, rim, places):
    c0, c1, c2 = (jnp.cos(angles[i]) for i in range(3))
    s0, s1, s2 = (jnp.sin(angles[i]) for i in range(3))
    frame = [
        c0 * c1 * c2 - s0 * s2, -(c0 * c1 * s2) - s0 * c2, c0 * s1,
        s0 * c1 * c2 + c0 * s2, -(s0 * c1 * s2) + c0 * c2, s0 * s1,
        -(s1 * c2), s1 * s2, c1,
    ]
    slots = source.shape[0]
    alive = jnp.arange(slots, dtype=jnp.int32) < live
    scaling = jnp.where(alive, weight, F32(0.0))
    inside = source < grains * places
    listed = jnp.maximum(source - grains * places, 0)
    group, within = listed // (rim * places), listed % (rim * places)
    source_place = jnp.where(inside, source // grains, within // rim)
    source_column = jnp.where(inside, source % grains, grains + group * rim + within % rim)
    target_place = jnp.where(alive, target // grains, -1)
    rows = frame + [scaling, source_place, source_column, target_place, target % grains]
    rows = [row.astype(F32) for row in rows] + [jnp.zeros((slots,), F32)] * (TABLE - len(rows))
    return jnp.stack(rows)


def rim_kernel(list_ref, own_ref, out_ref):
    rim, grains = list_ref.shape[0], own_ref.shape[2]
    width = own_ref.shape[1]
    step = padded(width)
    lanes = lax.broadcasted_iota(jnp.int32, (rim, grains), 1)
    pick = jnp.where(list_ref[...] == lanes, 1.0, 0.0).astype(BF16)
    out_ref[...] = jnp.zeros_like(out_ref)
    for c in range(3):
        found = lax.dot_general(pick, own_ref[c], NT, preferred_element_type=F32)
        out_ref[:, c * step : c * step + width] = found.astype(BF16)


def halo_kernel(sizes, rim_ref, table_ref, rims_ref, tables_ref, send_sem, recv_sem, own_sem):
    n_gx, n_gy, n_ha = sizes
    x, y, h = lax.axis_index("gx"), lax.axis_index("gy"), lax.axis_index("ha")
    beside = [(dx, dy) for dx in (-1, 0, 1) for dy in (-1, 0, 1) if (dx, dy) != (0, 0)]
    sends = []
    for dx, dy in beside:
        device = (lax.rem(x + dx + n_gx, n_gx), lax.rem(y + dy + n_gy, n_gy), h)
        slot = (1 - dx) * 3 + 1 - dy
        sends.append((device, rim_ref, rims_ref.at[slot], slot))
    for j in range(1, n_ha):
        device = (x, y, lax.rem(h + j, n_ha))
        sends.append((device, table_ref, tables_ref.at[h], 9 + j))
    barrier = pltpu.get_barrier_semaphore()
    for device, _, _, _ in sends:
        pl.semaphore_signal(barrier, inc=1, device_id=device, device_id_type=MESH)
    own = [
        pltpu.make_async_copy(rim_ref, rims_ref.at[4], own_sem.at[0]),
        pltpu.make_async_copy(table_ref, tables_ref.at[h], own_sem.at[1]),
    ]
    for copy in own:
        copy.start()
    pl.semaphore_wait(barrier, len(sends))
    copies = []
    for device, source, landing, slot in sends[::-1]:
        copy = pltpu.make_async_remote_copy(
            src_ref=source,
            dst_ref=landing,
            send_sem=send_sem.at[slot],
            recv_sem=recv_sem.at[slot],
            device_id=device,
            device_id_type=MESH,
        )
        copy.start()
        copies.append(copy)
    for copy in own:
        copy.wait()
    for copy in copies:
        copy.wait()


def ranks(mask):
    total, length = mask, mask.shape[1]
    lanes = lax.broadcasted_iota(jnp.int32, mask.shape, 1)
    step = 1
    while step < length:
        total = total + jnp.where(lanes >= step, pltpu.roll(total, step, 1), 0.0)
        step *= 2
    return total - mask


def table_row(tables_ref, row):
    return jnp.concatenate([tables_ref[j, row : row + 1, :] for j in range(tables_ref.shape[0])], axis=1)


def chosen(from_place, to_place, source, target, first, count):
    mask = jnp.where((from_place == source) & (to_place == target), 1.0, 0.0)
    key = jnp.where(mask > 0.0, ranks(mask) - first, -1.0)
    rows = lax.broadcasted_iota(jnp.int32, (count, mask.shape[1]), 0).astype(F32)
    return jnp.where(rows == key, 1.0, 0.0)


def route_kernel(round_ref, place_ref, tables_ref, own_ref, rims_ref, send_ref, mine_ref, most_ref):
    places = tables_ref.shape[0]
    width, grains = own_ref.shape[1:]
    count = mine_ref.shape[0]
    step = padded(width)
    first = (round_ref[0] * count).astype(F32)
    place = place_ref[0]
    here = place.astype(F32)
    from_place, to_place = table_row(tables_ref, SOURCE_PLACE), table_row(tables_ref, TARGET_PLACE)
    column_row = table_row(tables_ref, SOURCE_COLUMN) + 1.0
    own_lanes = lax.broadcasted_iota(jnp.int32, (count, grains), 1).astype(F32)
    rim_lanes = lax.broadcasted_iota(jnp.int32, (count, rims_ref.shape[0]), 1).astype(F32) + float(grains)
    for j in range(places):
        there = lax.rem(place + j, places).astype(F32)
        select = chosen(from_place, to_place, here, there, first, count)
        column = jnp.sum(select * column_row, axis=1, keepdims=True) - 1.0
        own_pick = jnp.where(own_lanes == column, 1.0, 0.0).astype(BF16)
        rim_pick = jnp.where(rim_lanes == column, 1.0, 0.0).astype(BF16)
        out = mine_ref if j == 0 else send_ref.at[j - 1]
        for c in range(3):
            a = lax.dot_general(own_pick, own_ref[c], NT, preferred_element_type=F32)
            b = jnp.dot(rim_pick, rims_ref[:, c * step : (c + 1) * step], preferred_element_type=F32)
            out[:, c * step : (c + 1) * step] = b.astype(BF16)
            out[:, c * step : c * step + width] = (a + b[:, :width]).astype(BF16)
    most = jnp.zeros((1, 1), F32)
    for source in range(places):
        for target in range(places):
            hit = jnp.where((from_place == float(source)) & (to_place == float(target)), 1.0, 0.0)
            most = jnp.maximum(most, jnp.sum(hit, axis=1, keepdims=True))
    most_ref[...] = jnp.broadcast_to(most, most_ref.shape)


def exchange_kernel(n_ha, send_ref, recv_ref, relay_ref, send_sem, recv_sem):
    x, y, h = lax.axis_index("gx"), lax.axis_index("gy"), lax.axis_index("ha")
    right, left = (x, y, lax.rem(h + 1, n_ha)), (x, y, lax.rem(h + n_ha - 1, n_ha))
    half = send_ref.shape[1] // 2
    upper, lower = pl.ds(0, half), pl.ds(half, half)
    barrier = pltpu.get_barrier_semaphore()
    for device in (right, left):
        pl.semaphore_signal(barrier, inc=1, device_id=device, device_id_type=MESH)
    pl.semaphore_wait(barrier, 2)

    def send(source, landing, device, slot):
        copy = pltpu.make_async_remote_copy(
            src_ref=source,
            dst_ref=landing,
            send_sem=send_sem.at[slot],
            recv_sem=recv_sem.at[slot],
            device_id=device,
            device_id_type=MESH,
        )
        copy.start()
        return copy

    across = [
        send(send_ref.at[1, upper], relay_ref.at[0], right, 0),
        send(send_ref.at[1, lower], relay_ref.at[1], left, 1),
    ]
    direct = [
        send(send_ref.at[0], recv_ref.at[0], right, 2),
        send(send_ref.at[2], recv_ref.at[2], left, 3),
    ]
    across[0].wait_recv()
    onward = [send(relay_ref.at[0], recv_ref.at[1, upper], right, 4)]
    across[1].wait_recv()
    onward.append(send(relay_ref.at[1], recv_ref.at[1, lower], left, 5))
    for copy in across:
        copy.wait_send()
    for copy in direct + onward:
        copy.wait()


def apply_kernel(
    opening, round_ref, place_ref, tables_ref, mine_ref, recv_ref, upsample_ref, normal_ref, tangent_ref,
    *rest,
):
    if opening:
        self_ref, own_ref, out_ref, pick_ref, rotated_ref = rest
    else:
        before_ref, out_ref, pick_ref, rotated_ref = rest
    places = tables_ref.shape[0]
    count = mine_ref.shape[0]
    nodes, width = upsample_ref.shape
    grains = out_ref.shape[2]
    step = padded(width)
    first = (round_ref[0] * count).astype(F32)
    place = place_ref[0]
    here = place.astype(F32)
    pick_ref[:count, :] = mine_ref[...]
    pick_ref[count:, :] = recv_ref[...]
    from_place, to_place = table_row(tables_ref, SOURCE_PLACE), table_row(tables_ref, TARGET_PLACE)
    every = jnp.concatenate([tables_ref[j] for j in range(places)], axis=1)
    picked_rows = []
    for j in range(places):
        there = lax.rem(place + places - j, places).astype(F32)
        picked_rows.append(chosen(from_place, to_place, there, here, first, count))
    select = jnp.concatenate(picked_rows, axis=0)
    table = lax.dot_general(select, every, NT, precision=lax.Precision.HIGHEST, preferred_element_type=F32)
    frame = [table[:, i : i + 1] for i in range(9)]

    def evaluate(begin, size):
        values = []
        for d in range(3):
            found = lax.dot_general(
                pick_ref[:, d * step : d * step + width],
                upsample_ref[pl.ds(begin, size), :],
                NT,
                preferred_element_type=F32,
            )
            values.append(found.astype(BF16).astype(F32))
        for c in range(3):
            turned = frame[3 * c] * values[0] + frame[3 * c + 1] * values[1] + frame[3 * c + 2] * values[2]
            rotated_ref[c, :, pl.ds(begin, size)] = turned.astype(BF16)

    tile = 256
    whole = nodes // tile

    def body(i, carry):
        evaluate(pl.multiple_of(i * tile, tile), tile)
        return carry

    lax.fori_loop(0, whole, body, 0)
    if nodes % tile:
        evaluate(whole * tile, nodes % tile)
    quad = [
        jnp.dot(rotated_ref[c], (normal_ref if c == 0 else tangent_ref)[...], preferred_element_type=F32)
        for c in range(3)
    ]
    scaling = table[:, SCALE : SCALE + 1]
    lanes = lax.broadcasted_iota(jnp.int32, (places * count, grains), 1).astype(F32)
    spot = jnp.where(lanes == table[:, TARGET_COLUMN : TARGET_COLUMN + 1], 1.0, 0.0).astype(BF16)
    for c in range(3):
        given = (frame[c] * quad[0] + frame[3 + c] * quad[1] + frame[6 + c] * quad[2]) * scaling
        high = given.astype(BF16)
        low = (given - high.astype(F32)).astype(BF16)
        total = lax.dot_general(high, spot, TN, preferred_element_type=F32)
        total += lax.dot_general(low, spot, TN, preferred_element_type=F32)
        if opening:
            total += jnp.dot(self_ref[...], own_ref[c], preferred_element_type=F32)
        else:
            total += before_ref[c]
        out_ref[c] = total


def shards(
    sizes,
    density,
    upsample,
    normal_kernel,
    tangent_kernel,
    self_operator,
    rim_list,
    pair_target,
    pair_source,
    pair_weight,
    pair_angles,
    live_count,
):
    places = sizes[2]
    width, grains = density.shape[1], density.shape[4]
    nodes = upsample.shape[0]
    rim = rim_list.shape[-1]
    slots = pair_source.shape[-1]
    span = 3 * padded(width)
    count = CAPACITY
    own = density.reshape(3, width, grains)
    normal, tangent = normal_kernel.T, tangent_kernel.T
    table = pair_table(
        pair_angles.reshape(3, slots),
        pair_weight.reshape(-1),
        pair_source.reshape(-1),
        pair_target.reshape(-1),
        live_count.reshape(()),
        grains,
        rim,
        places,
    )
    listed = pl.pallas_call(
        rim_kernel,
        out_shape=jax.ShapeDtypeStruct((rim, span), BF16),
        in_specs=[VMEM, VMEM],
        out_specs=VMEM,
        compiler_params=local_params(),
        name="rims",
    )(rim_list.reshape(rim, 1), own)
    rims, tables = pl.pallas_call(
        functools.partial(halo_kernel, sizes),
        out_shape=[
            jax.ShapeDtypeStruct((9, rim, span), BF16),
            jax.ShapeDtypeStruct((places, TABLE, slots), F32),
        ],
        in_specs=[ANY, ANY],
        out_specs=[ANY, ANY],
        scratch_shapes=[
            pltpu.SemaphoreType.DMA((9 + places,)),
            pltpu.SemaphoreType.DMA((9 + places,)),
            pltpu.SemaphoreType.DMA((2,)),
        ],
        compiler_params=pltpu.CompilerParams(collective_id=0, has_side_effects=True),
        name="halo",
    )(listed, table)
    rims = rims.reshape(9 * rim, span)
    place = lax.axis_index("ha").astype(jnp.int32).reshape(1)

    def route(turn):
        return pl.pallas_call(
            route_kernel,
            out_shape=[
                jax.ShapeDtypeStruct((places - 1, count, span), BF16),
                jax.ShapeDtypeStruct((count, span), BF16),
                jax.ShapeDtypeStruct((8, 128), F32),
            ],
            in_specs=[SMEM, SMEM, VMEM, VMEM, VMEM],
            out_specs=[VMEM, VMEM, VMEM],
            compiler_params=local_params(),
            name="route",
        )(turn, place, tables, own, rims)

    def exchange(send):
        return pl.pallas_call(
            functools.partial(exchange_kernel, places),
            out_shape=jax.ShapeDtypeStruct((places - 1, count, span), BF16),
            in_specs=[ANY],
            out_specs=ANY,
            scratch_shapes=[
                pltpu.VMEM((2, count // 2, span), BF16),
                pltpu.SemaphoreType.DMA((6,)),
                pltpu.SemaphoreType.DMA((6,)),
            ],
            compiler_params=pltpu.CompilerParams(collective_id=1, has_side_effects=True),
            name="exchange",
        )(send).reshape((places - 1) * count, span)

    def apply(turn, mine, received, before):
        opening = before is None
        last = [self_operator, own] if opening else [before]
        return pl.pallas_call(
            functools.partial(apply_kernel, opening),
            out_shape=jax.ShapeDtypeStruct((3, width, grains), F32),
            in_specs=[SMEM, SMEM] + [VMEM] * (6 + len(last)),
            out_specs=VMEM,
            scratch_shapes=[
                pltpu.VMEM((places * count, span), BF16),
                pltpu.VMEM((3, places * count, nodes), BF16),
            ],
            compiler_params=local_params(),
            name="apply",
        )(turn, place, tables, mine, received, upsample, normal, tangent, *last)

    turn = jnp.zeros((1,), jnp.int32)
    send, mine, most = route(turn)
    result = apply(turn, mine, exchange(send), None)
    rounds = (most[0, 0].astype(jnp.int32) + count - 1) // count

    def again(state):
        now, total = state
        send, mine, _ = route(now.reshape(1))
        return now + 1, apply(now.reshape(1), mine, exchange(send), total)

    _, result = lax.while_loop(lambda state: state[0] < rounds, again, (jnp.int32(1), result))
    return result.reshape(3, width, 1, 1, grains)


def solution(mesh):
    sizes = tuple(mesh.shape[axis] for axis in ("gx", "gy", "ha"))
    return jax.shard_map(
        functools.partial(shards, sizes),
        mesh=mesh,
        in_specs=(
            P(None, None, "gx", "gy", "ha"),
            P(),
            P(),
            P(),
            P(),
            P("gx", "gy", "ha"),
            P("gx", "gy", "ha", None),
            P("gx", "gy", "ha", None),
            P("gx", "gy", "ha", None),
            P(None, "gx", "gy", "ha", None),
            P("gx", "gy", "ha"),
        ),
        out_specs=P(None, None, "gx", "gy", "ha"),
        check_vma=False,
    )
```

time: 317 us -> 87.4 us (0.28)
  waiting for transfers between devices: 110 us -> 0 us
  local copies, waits for them, and re-layouts: 89.6 us -> 8.57 us
  Pallas kernels: 0 us -> 74.8 us
  other arithmetic: 62.5 us -> 2.39 us
  matrix products: 15.8 us -> 0 us
  between operations: 14.4 us -> 1.28 us
  blocking collectives: 12.5 us -> 0 us
  starting transfers between devices: 9.99 us -> 0 us
    reduce_scatter x1 -> x0, waiting for transfers between devices: 75.5 us -> none  [shards(): lax.psum_scatter(partial_value, 'ha', scatter_dimension=2, tiled=True)]
    pallas_call x0 -> x5, Pallas kernels: none -> 74.8 us  [the longest x1 27.8 us: shards(): pl.pallas_call(functools.partial(halo_kernel, sizes), out_shape=[jax.Shap...]
    ppermute x4 -> x0, waiting for transfers between devices: 33.6 us -> none  [the longest x2 26.1 us: with_halo(): lax.ppermute(head, axis, [((i + 1) % count, i) for i in range(count)])]
    scatter-add x1 -> x0, other arithmetic: 31.4 us -> none  [shards(): jnp.zeros((3, width, slab_total), jnp.float32).at[:, :, target]]
    concatenate x3 -> x0, other arithmetic: 23.2 us -> none  [the longest x1 17.9 us: shards(): jnp.concatenate([slab_data, beside_all.reshape(3, slab_data.shape[1], -1)...]
    reshape x2, local copies, waits for them, and re-layouts: 21.5 us -> 5.44 us  [the longest x1 4.11 us: shards(): return result.reshape(3, width, 1, 1, grains)]
    dot_general x6 -> x0, matrix products: 15.8 us -> none  [the longest x2 6.25 us: rotation(): jnp.einsum('abp,bcp,cdp->adp', about_z(first), tilt, about_z(third), prec...]
    all_gather x1 -> x0, blocking collectives: 12.5 us -> none  [spread(): lax.all_gather(rim_data, 'ha', axis=2, tiled=True)]
  transfers between devices with their start and end apart: 6 -> 0, of which waited for: 3 -> 0; matrix products, arithmetic and copies ran while one was open for 20% -> 0% of each run, Pallas kernels for 0% -> 0%
where the time goes in v1:
time: 87.4 us; the launch traced here: 87.1 us
  Pallas kernels  74.8 us (86%)
  local copies, waits for them, and re-layouts  8.57 us (10%)
  other arithmetic  2.39 us (3%)
  between operations  1.28 us (1%)
    pallas_call x1, Pallas kernels, shards(): pl.pallas_call(functools.partial(halo_kernel, sizes), out_shape=[jax.Shap...  27.8 us
    pallas_call x1, Pallas kernels, apply(): pl.pallas_call(functools.partial(apply_kernel, opening), out_shape=jax.Sh...  20.5 us
    pallas_call x1, Pallas kernels, exchange(): pl.pallas_call(functools.partial(exchange_kernel, places), out_shape=jax....  18.3 us
    pallas_call x1, Pallas kernels, route(): pl.pallas_call(route_kernel, out_shape=[jax.ShapeDtypeStruct((places - 1,...  5.91 us
    reshape x1, local copies, waits for them, and re-layouts, shards(): return result.reshape(3, width, 1, 1, grains)  4.11 us
    pallas_call x1, Pallas kernels, shards(): pl.pallas_call(rim_kernel, out_shape=jax.ShapeDtypeStruct((rim, span), BF...  2.28 us

profile of v1, /device:TPU:1, one launch (start us, length us, event | category | flops | bytes accessed | tf_op | source)
XLA Modules:
  0.0 87.1 jit_solution(17541546786388442854)
XLA Ops:
  0.7 0.8 bitcast_multiply_fusion
  1.5 0.7 fusion.3
  2.2 0.7 cosine_bitcast_fusion
  3.0 0.8 fusion.9
  3.8 1.2 %stack.5.table_ref = f32[16,256]{1,0:T(8,128)} concatenate(f32[1,256]{1,0:T(1,128)S(1)} %get-tuple-element.97, f32[1,256]{1,0:T(1,128)S(1)} %get-tuple-element.96, f32[1,256]{1,0:T(1,128)S(1)} %get-tuple-element.95, f32[1,256]{1,0:T(1,128)S(1)} %fusion.9, f32[1,256]{1,0:T(1,128)S(1)} %get-tuple-element.94, f32[1,256]{1,0:T(1,128)S(1)} %get-tuple-element.93, ...), dimensions={0} | concatenate | bytes 32768 | tf_op jit(solution)/shard_map/stack | solution.py:50
  5.0 1.3 %copy.12.list_ref = s32[32,1]{1,0:T(8,128)} copy(s32[32,1]{0,1:T(1,128)} %bitcast.149) | data formatting | bytes 256 | tf_op jit(solution)/shard_map/reshape | solution.py:310
  6.4 2.3 %rims.1.rim_ref = bf16[32,1920]{1,0:T(8,128)(2,1)} custom-call(s32[32,1]{1,0:T(8,128)} %copy.12.list_ref, bf16[3,625,256]{2,1,0:T(8,128)(2,1)} %bitcast.142), custom_call_target="tpu_custom_call" | custom-call | tf_op jit(solution)/shard_map/rims/pallas_call | solution.py:303
  8.6 27.8 %halo.1 = (bf16[9,32,1920]{2,1,0:T(8,128)(2,1)}, f32[4,16,256]{2,1,0:T(8,128)S(1)}) custom-call(bf16[32,1920]{1,0:T(8,128)(2,1)} %rims.1.rim_ref, f32[16,256]{1,0:T(8,128)} %stack.5.table_ref), custom_call_target="tpu_custom_call" | custom-call | tf_op jit(solution)/shard_map/halo/pallas_call | solution.py:311
  36.5 0.0 copy-start
  36.5 5.9 %route.2 = (bf16[3,96,1920]{2,1,0:T(8,128)(2,1)}, bf16[96,1920]{1,0:T(8,128)(2,1)}, f32[8,128]{1,0:T(8,128)}) custom-call(s32[1]{0:T(128)} %constant.101.clone.1.round_ref, s32[1]{0:T(128)} %bitcast.2.place_ref, f32[4,16,256]{2,1,0:T(8,128)S(1)} %get-tuple-element.175.tables_ref, bf16[3,625,256]{2,1,0:T(8,128)(2,1)} %bitcast.143, bf16[288,1920]{1,0:T(8,128)(2,1)} %bitcast.146), custom_call_target="tpu_custom_call" | custom-call | tf_op jit(solution)/shard_map/route/pallas_call | solution.py:331
  42.4 1.2 %slice.21 = f32[1,1]{1,0:T(1,128)} slice(f32[8,128]{1,0:T(8,128)} %get-tuple-element.69), slice={[0:1], [0:1]} | slice | bytes 8 | tf_op jit(solution)/shard_map/slice | solution.py:378
  44.1 18.3 %exchange.2 = bf16[3,96,1920]{2,1,0:T(8,128)(2,1)} custom-call(bf16[3,96,1920]{2,1,0:T(8,128)(2,1)} %get-tuple-element.68.send_ref), custom_call_target="tpu_custom_call" | custom-call | tf_op jit(solution)/shard_map/exchange/pallas_call | solution.py:345
  62.4 0.0 copy-done
  62.4 20.5 %apply.2 = f32[3,625,256]{2,1,0:T(8,128)} custom-call(s32[1]{0:T(128)} %constant.101.clone.1.round_ref, s32[1]{0:T(128)} %bitcast.2.place_ref, f32[4,16,256]{2,1,0:T(8,128)S(1)} %get-tuple-element.175.tables_ref, bf16[96,1920]{1,0:T(8,128)(2,1)} %get-tuple-element.67.mine_ref, bf16[288,1920]{1,0:T(8,128)(2,1)} %bitcast.148, bf16[2112,625]{1,0:T(8,128)(2,1)S(1)} %copy-done, ...), custom_call_target="tpu_custom_call" | custom-call | tf_op jit(solution)/shard_map/apply/pallas_call | solution.py:362
  83.0 4.1 %reshape.659 = f32[3,625,1,1,256]{4,3,2,1,0:T(1,128)} reshape(f32[3,625,256]{2,1,0:T(8,128)} %get-tuple-element.70) | data formatting | bytes 3840000 | tf_op jit(solution)/shard_map/reshape | solution.py:386
  (2 shorter events, 0.0 us)
Async XLA Ops:
  36.5 25.9 %copy-start = (bf16[2112,625]{1,0:T(8,128)(2,1)S(1)}, bf16[2112,625]{1,0:T(8,128)(2,1)}, u32[]{:S(2)}) copy-start(bf16[2112,625]{1,0:T(8,128)(2,1)} %upsample_ref.1) | copy-start | bytes 7920004

commit v2 on v1

v2 whole, which is shorter than its diff:
```python
import functools

import jax
import jax.numpy as jnp
from jax import lax
from jax.experimental import pallas as pl
from jax.experimental.pallas import tpu as pltpu
from jax.sharding import PartitionSpec as P

MESH = pl.DeviceIdType.MESH
ANY = pl.BlockSpec(memory_space=pl.ANY)
VMEM = pl.BlockSpec(memory_space=pltpu.VMEM)
SMEM = pl.BlockSpec(memory_space=pltpu.SMEM)
CAPACITY = 96
TABLE = 16
SCALE, SOURCE_PLACE, SOURCE_COLUMN, TARGET_PLACE, TARGET_COLUMN = 9, 10, 11, 12, 13
NT = (((1,), (1,)), ((), ()))
TN = (((0,), (0,)), ((), ()))
F32 = jnp.float32
BF16 = jnp.bfloat16


def padded(width):
    return (width + 127) // 128 * 128


def limit(mebibytes, **others):
    return pltpu.CompilerParams(vmem_limit_bytes=mebibytes * 1024 * 1024, **others)


def split(value, size):
    bits = size.bit_length() - 1
    assert size == 1 << bits
    return lax.shift_right_logical(value, bits), value & (size - 1)


def prepare_kernel(places, live_ref, list_ref, target_ref, source_ref, weight_ref, angles_ref, own_ref, rim_ref, table_ref):
    width, grains = own_ref.shape[1:]
    rim, slots = list_ref.shape[1], source_ref.shape[1]
    step = padded(width)
    square = [lax.broadcasted_iota(jnp.int32, (rim, rim), axis) for axis in (0, 1)]
    listed = jnp.where(square[0] == square[1], list_ref[...].astype(F32), 0.0)
    listed = jnp.sum(listed, axis=1, keepdims=True)
    lanes = lax.broadcasted_iota(jnp.int32, (rim, grains), 1).astype(F32)
    pick = jnp.where(listed == lanes, 1.0, 0.0).astype(BF16)
    rim_ref[...] = jnp.zeros_like(rim_ref)
    for c in range(3):
        found = lax.dot_general(pick, own_ref[c], NT, preferred_element_type=F32)
        rim_ref[:, c * step : c * step + width] = found.astype(BF16)
    c0, c1, c2 = (jnp.cos(angles_ref[i]) for i in range(3))
    s0, s1, s2 = (jnp.sin(angles_ref[i]) for i in range(3))
    frame = [
        c0 * c1 * c2 - s0 * s2, -(c0 * c1 * s2) - s0 * c2, c0 * s1,
        s0 * c1 * c2 + c0 * s2, -(s0 * c1 * s2) + c0 * c2, s0 * s1,
        -(s1 * c2), s1 * s2, c1,
    ]
    alive = lax.broadcasted_iota(jnp.int32, (1, slots), 1) < live_ref[0]
    source = source_ref[...]
    inside = source < grains * places
    place, column = split(source, grains)
    group, within = split(jnp.maximum(source - grains * places, 0), rim * places)
    rim_place, rim_column = split(within, rim)
    target_place, target_column = split(target_ref[...], grains)
    rows = frame + [
        jnp.where(alive, weight_ref[...], 0.0),
        jnp.where(inside, place, rim_place).astype(F32),
        jnp.where(inside, column, grains + group * rim + rim_column).astype(F32),
        jnp.where(alive, target_place, -1).astype(F32),
        target_column.astype(F32),
    ]
    table_ref[...] = jnp.zeros_like(table_ref)
    for i, row in enumerate(rows):
        table_ref[i : i + 1, :] = row


def gather_kernel(
    sizes, rim_ref, table_ref, own_ref, self_ref, rims_ref, tables_ref, send_ref, mine_ref, most_ref, base_ref,
    send_sem, recv_sem, own_sem,
):
    n_gx, n_gy, n_ha = sizes
    x, y, h = lax.axis_index("gx"), lax.axis_index("gy"), lax.axis_index("ha")
    near = 1 - 2 * lax.rem(y, 2)
    partner = (x, y + near, h)
    far = lax.rem(y - near + n_gy, n_gy)
    barrier = pltpu.get_barrier_semaphore()
    mates = [(x, y, lax.rem(h + j, n_ha)) for j in range(1, n_ha)]
    sides = [(lax.rem(x + dx + n_gx, n_gx), y, h) for dx in (-1, 1)]
    beyond = [(lax.rem(x + dx + n_gx, n_gx), far, h) for dx in (-1, 0, 1)]
    peers = mates + sides + beyond + [partner]
    for device in peers:
        pl.semaphore_signal(barrier, inc=1, device_id=device, device_id_type=MESH)
    own = [
        pltpu.make_async_copy(rim_ref, rims_ref.at[4], own_sem.at[0]),
        pltpu.make_async_copy(table_ref, tables_ref.at[h], own_sem.at[1]),
    ]
    for copy in own:
        copy.start()
    pl.semaphore_wait(barrier, len(peers))

    def send(source, landing, device, slot):
        copy = pltpu.make_async_remote_copy(
            src_ref=source,
            dst_ref=landing,
            send_sem=send_sem.at[slot],
            recv_sem=recv_sem.at[slot],
            device_id=device,
            device_id_type=MESH,
        )
        copy.start()
        return copy

    tables = [send(table_ref, tables_ref.at[h], mates[j], j) for j in range(n_ha - 1)]
    aside = [send(rim_ref, rims_ref.at[(1 - dx) * 3 + 1], sides[(dx + 1) // 2], n_ha + dx) for dx in (-1, 1)]
    rest = [
        send(rim_ref, rims_ref.at[(1 - dx) * 3 + 1 + near], beyond[dx + 1], n_ha + 3 + dx) for dx in (-1, 0, 1)
    ]
    rest.append(send(rim_ref, rims_ref.at[4 - near], partner, n_ha))
    for c in range(3):
        base_ref[c] = jnp.dot(self_ref[...], own_ref[c], preferred_element_type=F32)
    for copy in own:
        copy.wait()
    for copy in tables:
        copy.wait()
    columns = route_columns(jnp.float32(0.0), h, tables_ref, mine_ref.shape[0])
    outs = [mine_ref] + [send_ref.at[j] for j in range(n_ha - 1)]
    for column, out in zip(columns, outs):
        pick_own(column, own_ref, out)
    most_ref[...] = jnp.broadcast_to(longest(tables_ref), most_ref.shape)
    for i, dx in enumerate((-1, 1)):
        aside[i].wait_recv()
        rest.append(
            send(rims_ref.at[(1 - dx) * 3 + 1], rims_ref.at[(1 - dx) * 3 + 1 - near], partner, n_ha + 5 + i)
        )
    for copy in aside:
        copy.wait_send()
    for copy in rest:
        copy.wait()
    for column, out in zip(columns, outs):
        add_listed(column, rims_ref, own_ref.shape[2], out)


def ranks(mask):
    total, length = mask, mask.shape[1]
    lanes = lax.broadcasted_iota(jnp.int32, mask.shape, 1)
    step = 1
    while step < length:
        total = total + jnp.where(lanes >= step, pltpu.roll(total, step, 1), 0.0)
        step *= 2
    return total - mask


def table_row(tables_ref, row):
    return jnp.concatenate([tables_ref[j, row : row + 1, :] for j in range(tables_ref.shape[0])], axis=1)


def chosen(from_place, to_place, source, target, first, count):
    mask = jnp.where((from_place == source) & (to_place == target), 1.0, 0.0)
    key = jnp.where(mask > 0.0, ranks(mask) - first, -1.0)
    rows = lax.broadcasted_iota(jnp.int32, (count, mask.shape[1]), 0).astype(F32)
    return jnp.where(rows == key, 1.0, 0.0)


def route_columns(first, place, tables_ref, count):
    places = tables_ref.shape[0]
    here = place.astype(F32)
    from_place, to_place = table_row(tables_ref, SOURCE_PLACE), table_row(tables_ref, TARGET_PLACE)
    column_row = table_row(tables_ref, SOURCE_COLUMN) + 1.0
    columns = []
    for j in range(places):
        there = lax.rem(place + j, places).astype(F32)
        select = chosen(from_place, to_place, here, there, first, count)
        columns.append(jnp.sum(select * column_row, axis=1, keepdims=True) - 1.0)
    return columns


def longest(tables_ref):
    places = tables_ref.shape[0]
    from_place, to_place = table_row(tables_ref, SOURCE_PLACE), table_row(tables_ref, TARGET_PLACE)
    most = jnp.zeros((1, 1), F32)
    for source in range(places):
        for target in range(places):
            hit = jnp.where((from_place == float(source)) & (to_place == float(target)), 1.0, 0.0)
            most = jnp.maximum(most, jnp.sum(hit, axis=1, keepdims=True))
    return most


def pick_own(column, own_ref, out):
    count, (width, grains) = column.shape[0], own_ref.shape[1:]
    step = padded(width)
    lanes = lax.broadcasted_iota(jnp.int32, (count, grains), 1).astype(F32)
    pick = jnp.where(lanes == column, 1.0, 0.0).astype(BF16)
    out[...] = jnp.zeros(out.shape, BF16)
    for c in range(3):
        found = lax.dot_general(pick, own_ref[c], NT, preferred_element_type=F32)
        out[:, c * step : c * step + width] = found.astype(BF16)


def add_listed(column, rims_ref, grains, out):
    count, groups, rim = column.shape[0], rims_ref.shape[0], rims_ref.shape[1]
    lanes = lax.broadcasted_iota(jnp.int32, (count, groups * rim), 1).astype(F32) + float(grains)
    pick = jnp.where(lanes == column, 1.0, 0.0).astype(BF16)
    rims = rims_ref[...].reshape(groups * rim, rims_ref.shape[2])
    found = jnp.dot(pick, rims, preferred_element_type=F32)
    out[...] = (out[...].astype(F32) + found).astype(BF16)


def route_kernel(round_ref, place_ref, tables_ref, own_ref, rims_ref, send_ref, mine_ref):
    count = mine_ref.shape[0]
    columns = route_columns((round_ref[0] * count).astype(F32), place_ref[0], tables_ref, count)
    for column, out in zip(columns, [mine_ref] + [send_ref.at[j] for j in range(send_ref.shape[0])]):
        pick_own(column, own_ref, out)
        add_listed(column, rims_ref, own_ref.shape[2], out)


def exchange_kernel(n_ha, send_ref, recv_ref, relay_ref, send_sem, recv_sem):
    x, y, h = lax.axis_index("gx"), lax.axis_index("gy"), lax.axis_index("ha")
    right, left = (x, y, lax.rem(h + 1, n_ha)), (x, y, lax.rem(h + n_ha - 1, n_ha))
    half = send_ref.shape[1] // 2
    upper, lower = pl.ds(0, half), pl.ds(half, half)
    barrier = pltpu.get_barrier_semaphore()
    for device in (right, left):
        pl.semaphore_signal(barrier, inc=1, device_id=device, device_id_type=MESH)
    pl.semaphore_wait(barrier, 2)

    def send(source, landing, device, slot):
        copy = pltpu.make_async_remote_copy(
            src_ref=source,
            dst_ref=landing,
            send_sem=send_sem.at[slot],
            recv_sem=recv_sem.at[slot],
            device_id=device,
            device_id_type=MESH,
        )
        copy.start()
        return copy

    across = [
        send(send_ref.at[1, upper], relay_ref.at[0], right, 0),
        send(send_ref.at[1, lower], relay_ref.at[1], left, 1),
    ]
    direct = [
        send(send_ref.at[0], recv_ref.at[0], right, 2),
        send(send_ref.at[2], recv_ref.at[2], left, 3),
    ]
    across[0].wait_recv()
    onward = [send(relay_ref.at[0], recv_ref.at[1, upper], right, 4)]
    across[1].wait_recv()
    onward.append(send(relay_ref.at[1], recv_ref.at[1, lower], left, 5))
    for copy in across:
        copy.wait_send()
    for copy in direct + onward:
        copy.wait()


def apply_kernel(
    opening, round_ref, place_ref, tables_ref, mine_ref, recv_ref, upsample_ref, normal_ref, tangent_ref,
    before_ref, out_ref, pick_ref, rotated_ref,
):
    places = tables_ref.shape[0]
    count = mine_ref.shape[0]
    nodes, width = upsample_ref.shape
    lines = out_ref.shape[0] // (3 * width)
    grains = lines * 128
    step = padded(width)
    first = (round_ref[0] * count).astype(F32)
    place = place_ref[0]
    here = place.astype(F32)
    pick_ref[:count, :] = mine_ref[...]
    pick_ref[count:, :] = recv_ref[...]
    from_place, to_place = table_row(tables_ref, SOURCE_PLACE), table_row(tables_ref, TARGET_PLACE)
    every = jnp.concatenate([tables_ref[j] for j in range(places)], axis=1)
    picked_rows = []
    for j in range(places):
        there = lax.rem(place + places - j, places).astype(F32)
        picked_rows.append(chosen(from_place, to_place, there, here, first, count))
    select = jnp.concatenate(picked_rows, axis=0)
    table = lax.dot_general(select, every, NT, precision=lax.Precision.HIGHEST, preferred_element_type=F32)
    frame = [table[:, i : i + 1] for i in range(9)]

    def evaluate(begin, size):
        values = []
        for d in range(3):
            found = lax.dot_general(
                pick_ref[:, d * step : d * step + width],
                upsample_ref[pl.ds(begin, size), :],
                NT,
                preferred_element_type=F32,
            )
            values.append(found.astype(BF16).astype(F32))
        for c in range(3):
            turned = frame[3 * c] * values[0] + frame[3 * c + 1] * values[1] + frame[3 * c + 2] * values[2]
            rotated_ref[c, :, pl.ds(begin, size)] = turned.astype(BF16)

    tile = 256
    whole = nodes // tile

    def body(i, carry):
        evaluate(pl.multiple_of(i * tile, tile), tile)
        return carry

    lax.fori_loop(0, whole, body, 0)
    if nodes % tile:
        evaluate(whole * tile, nodes % tile)
    quad = [
        jnp.dot(rotated_ref[c], (normal_ref if c == 0 else tangent_ref)[...], preferred_element_type=F32)
        for c in range(3)
    ]
    scaling = table[:, SCALE : SCALE + 1]
    lanes = lax.broadcasted_iota(jnp.int32, (places * count, grains), 1).astype(F32)
    spot = jnp.where(lanes == table[:, TARGET_COLUMN : TARGET_COLUMN + 1], 1.0, 0.0).astype(BF16)
    for c in range(3):
        given = (frame[c] * quad[0] + frame[3 + c] * quad[1] + frame[6 + c] * quad[2]) * scaling
        high = given.astype(BF16)
        low = (given - high.astype(F32)).astype(BF16)
        total = lax.dot_general(high, spot, TN, preferred_element_type=F32)
        total += lax.dot_general(low, spot, TN, preferred_element_type=F32)
        for line in range(lines):
            spread = pl.ds(c * width * lines + line, width, stride=lines)
            part = slice(line * 128, (line + 1) * 128)
            before = before_ref[c, :, part] if opening else before_ref[spread, :]
            out_ref[spread, :] = total[:, part] + before


def shards(
    sizes,
    density,
    upsample,
    normal_kernel,
    tangent_kernel,
    self_operator,
    rim_list,
    pair_target,
    pair_source,
    pair_weight,
    pair_angles,
    live_count,
):
    places = sizes[2]
    width, grains = density.shape[1], density.shape[4]
    nodes = upsample.shape[0]
    rim = rim_list.shape[-1]
    slots = pair_source.shape[-1]
    span = 3 * padded(width)
    count = CAPACITY
    own = density.reshape(3, width, grains)
    normal, tangent = normal_kernel.T, tangent_kernel.T
    lines = grains // 128
    listed, table = pl.pallas_call(
        functools.partial(prepare_kernel, places),
        out_shape=[jax.ShapeDtypeStruct((rim, span), BF16), jax.ShapeDtypeStruct((TABLE, slots), F32)],
        in_specs=[SMEM] + [VMEM] * 6,
        out_specs=[VMEM, VMEM],
        compiler_params=limit(8),
        name="prepare",
    )(
        live_count.reshape(1),
        rim_list.reshape(1, rim),
        pair_target.reshape(1, slots),
        pair_source.reshape(1, slots),
        pair_weight.reshape(1, slots),
        pair_angles.reshape(3, 1, slots),
        own,
    )
    rims, tables, send, mine, most, base = pl.pallas_call(
        functools.partial(gather_kernel, sizes),
        out_shape=[
            jax.ShapeDtypeStruct((9, rim, span), BF16),
            jax.ShapeDtypeStruct((places, TABLE, slots), F32),
            jax.ShapeDtypeStruct((places - 1, count, span), BF16),
            jax.ShapeDtypeStruct((count, span), BF16),
            jax.ShapeDtypeStruct((1, 128), F32),
            jax.ShapeDtypeStruct((3, width, grains), F32),
        ],
        in_specs=[ANY, ANY, VMEM, VMEM],
        out_specs=[VMEM] * 6,
        scratch_shapes=[
            pltpu.SemaphoreType.DMA((places + 7,)),
            pltpu.SemaphoreType.DMA((places + 7,)),
            pltpu.SemaphoreType.DMA((2,)),
        ],
        compiler_params=limit(24, collective_id=0, has_side_effects=True),
        name="gather",
    )(listed, table, own, self_operator)
    place = lax.axis_index("ha").astype(jnp.int32).reshape(1)

    def route(turn):
        return pl.pallas_call(
            route_kernel,
            out_shape=[
                jax.ShapeDtypeStruct((places - 1, count, span), BF16),
                jax.ShapeDtypeStruct((count, span), BF16),
            ],
            in_specs=[SMEM, SMEM, VMEM, VMEM, VMEM],
            out_specs=[VMEM, VMEM],
            compiler_params=limit(24),
            name="route",
        )(turn, place, tables, own, rims)

    def exchange(send):
        return pl.pallas_call(
            functools.partial(exchange_kernel, places),
            out_shape=jax.ShapeDtypeStruct((places - 1, count, span), BF16),
            in_specs=[ANY],
            out_specs=ANY,
            scratch_shapes=[
                pltpu.VMEM((2, count // 2, span), BF16),
                pltpu.SemaphoreType.DMA((6,)),
                pltpu.SemaphoreType.DMA((6,)),
            ],
            compiler_params=limit(4, collective_id=1, has_side_effects=True),
            name="exchange",
        )(send).reshape((places - 1) * count, span)

    def apply(turn, mine, received, before, opening):
        return pl.pallas_call(
            functools.partial(apply_kernel, opening),
            out_shape=jax.ShapeDtypeStruct((3 * width * lines, 128), F32),
            in_specs=[SMEM, SMEM] + [VMEM] * 7,
            out_specs=VMEM,
            scratch_shapes=[
                pltpu.VMEM((places * count, span), BF16),
                pltpu.VMEM((3, places * count, nodes), BF16),
            ],
            compiler_params=limit(40),
            name="apply",
        )(turn, place, tables, mine, received, upsample, normal, tangent, before)

    turn = jnp.zeros((1,), jnp.int32)
    result = apply(turn, mine, exchange(send), base, True)
    rounds = (most[0, 0].astype(jnp.int32) + count - 1) // count

    def again(state):
        now, total = state
        send, mine = route(now.reshape(1))
        return now + 1, apply(now.reshape(1), mine, exchange(send), total, False)

    _, result = lax.while_loop(lambda state: state[0] < rounds, again, (jnp.int32(1), result))
    return result.reshape(3, width, 1, 1, grains)


def solution(mesh):
    sizes = tuple(mesh.shape[axis] for axis in ("gx", "gy", "ha"))
    return jax.shard_map(
        functools.partial(shards, sizes),
        mesh=mesh,
        in_specs=(
            P(None, None, "gx", "gy", "ha"),
            P(),
            P(),
            P(),
            P(),
            P("gx", "gy", "ha"),
            P("gx", "gy", "ha", None),
            P("gx", "gy", "ha", None),
            P("gx", "gy", "ha", None),
            P(None, "gx", "gy", "ha", None),
            P("gx", "gy", "ha"),
        ),
        out_specs=P(None, None, "gx", "gy", "ha"),
        check_vma=False,
    )
```

time: 87.4 us -> 77.1 us (0.88)
  Pallas kernels: 74.8 us -> 65.1 us
  other arithmetic: 2.39 us -> 0 us
  local copies, waits for them, and re-layouts: 8.57 us -> 10.8 us
    pallas_call x3 -> x2, Pallas kernels: 36 us -> 28.3 us  [the longest x1 26.7 us: shards(): pl.pallas_call(functools.partial(gather_kernel, sizes), out_shape=[jax.Sh...]
    unnamed x2 -> x16, local copies, waits for them, and re-layouts: 0.01 us -> 6.74 us
    reshape x1 -> x0, local copies, waits for them, and re-layouts: 1.33 us -> none  [shards(): rim_list.reshape(rim, 1)]
    another operation x2 -> x0, local copies, waits for them, and re-layouts: 1.24 us -> none  [pair_table(): return jnp.stack(rows)]
    pallas_call x1, Pallas kernels: 18.3 us -> 17.1 us  [exchange(): pl.pallas_call(functools.partial(exchange_kernel, places), out_shape=jax....]
    slice x1 -> x0, local copies, waits for them, and re-layouts: 1.16 us -> none  [shards(): rounds = (most[0, 0].astype(jnp.int32) + count - 1) // count]
where the time goes in v2:
time: 77.1 us; the launch traced here: 76.7 us
  Pallas kernels  65.1 us (84%)
  local copies, waits for them, and re-layouts  10.8 us (14%)
    pallas_call x1, Pallas kernels, shards(): pl.pallas_call(functools.partial(gather_kernel, sizes), out_shape=[jax.Sh...  26.7 us
    pallas_call x1, Pallas kernels, apply(): pl.pallas_call(functools.partial(apply_kernel, opening), out_shape=jax.Sh...  19.8 us
    pallas_call x1, Pallas kernels, exchange(): pl.pallas_call(functools.partial(exchange_kernel, places), out_shape=jax....  17.1 us
    unnamed x16, local copies, waits for them, and re-layouts  6.74 us
    reshape x1, local copies, waits for them, and re-layouts, shards(): return result.reshape(3, width, 1, 1, grains)  4.04 us
    pallas_call x1, Pallas kernels, shards(): pl.pallas_call(functools.partial(prepare_kernel, places), out_shape=[jax....  1.62 us

profile of v2, /device:TPU:1, one launch (start us, length us, event | category | flops | bytes accessed | tf_op | source)
XLA Modules:
  0.0 76.7 jit_solution(3992842004678850811)
XLA Ops:
  0.7 0.0 copy-start.3
  0.7 0.7 copy-done.3
  1.3 0.0 copy-start.4
  1.3 0.7 copy-done.4
  2.0 0.0 copy-start.5
  2.0 0.7 copy-done.5
  2.7 0.0 copy-start.6
  2.7 0.7 copy-done.6
  3.4 0.0 copy-start.7
  3.4 0.7 copy-done.7
  4.0 1.6 %prepare.1 = (bf16[32,1920]{1,0:T(8,128)(2,1)S(1)}, f32[16,256]{1,0:T(8,128)S(1)}) custom-call(s32[1]{0:T(128)} %bitcast.20.live_ref, s32[1,32]{1,0:T(1,128)S(1)} %bitcast.27, s32[1,256]{1,0:T(1,128)S(1)} %bitcast.24, s32[1,256]{1,0:T(1,128)S(1)} %bitcast.25, f32[1,256]{1,0:T(1,128)S(1)} %bitcast.26, f32[3,1,256]{2,1,0:T(1,128)S(1)} %bitcast.23, ...), custom_call_target="tpu_custom_call" | custom-call | tf_op jit(solution)/shard_map/prepare/pallas_call | solution.py:348
  5.6 0.0 copy-start.2
  5.6 1.2 %copy-done.2 = bf16[625,625]{1,0:T(8,128)(2,1)S(1)} copy-done((bf16[625,625]{1,0:T(8,128)(2,1)S(1)}, bf16[625,625]{1,0:T(8,128)(2,1)}, u32[]{:S(2)}) %copy-start.2) | copy-done | bytes 781274
  6.8 26.7 %gather.1 = (bf16[9,32,1920]{2,1,0:T(8,128)(2,1)}, f32[4,16,256]{2,1,0:T(8,128)S(1)}, bf16[3,96,1920]{2,1,0:T(8,128)(2,1)S(1)}, bf16[96,1920]{1,0:T(8,128)(2,1)S...) custom-call(bf16[32,1920]{1,0:T(8,128)(2,1)S(1)} %get-tuple-element.68.rim_ref, ...), custom_call_target="tpu_custom_call" | custom-call | tf_op jit(solution)/shard_map/gather/pallas_call | solution.py:364
  33.5 0.0 copy-start
  33.5 1.0 %copy-done = bf16[3,96,1920]{2,1,0:T(8,128)(2,1)} copy-done((bf16[3,96,1920]{2,1,0:T(8,128)(2,1)}, bf16[3,96,1920]{2,1,0:T(8,128)(2,1)S(1)}, u32[]{:S(2)}) %copy-start) | copy-done | bytes 1105944
  34.6 0.0 copy-start.1
  34.6 1.2 %copy-done.1 = bf16[3,96,1920]{2,1,0:T(8,128)(2,1)S(1)} copy-done((bf16[3,96,1920]{2,1,0:T(8,128)(2,1)S(1)}, bf16[3,96,1920]{2,1,0:T(8,128)(2,1)}, u32[]{:S(2)}) %copy-start.1) | copy-done | bytes 1105944
  35.8 17.1 %exchange.2 = bf16[3,96,1920]{2,1,0:T(8,128)(2,1)S(1)} custom-call(bf16[3,96,1920]{2,1,0:T(8,128)(2,1)S(1)} %copy-done.1), custom_call_target="tpu_custom_call" | custom-call | tf_op jit(solution)/shard_map/exchange/pallas_call | solution.py:400
  52.9 19.8 %apply.2 = f32[3750,128]{1,0:T(8,128)} custom-call(s32[1]{0:T(128)} %constant.22.clone.1.round_ref, s32[1]{0:T(128)} %bitcast.2.place_ref, f32[4,16,256]{2,1,0:T(8,128)S(1)} %get-tuple-element.167.tables_ref, bf16[96,1920]{1,0:T(8,128)(2,1)S(1)} %get-tuple-element.71.mine_ref, bf16[288,1920]{1,0:T(8,128)(2,1)S(1)} %bitcast.22, ...), custom_call_target="tpu_custom_call" | custom-call | tf_op jit(solution)/shard_map/apply/pallas_call | solution.py:415
  72.7 4.0 %reshape.58 = f32[3,625,1,1,256]{4,3,2,1,0:T(1,128)} reshape(f32[3750,128]{1,0:T(8,128)} %get-tuple-element.76) | data formatting | bytes 3840000 | tf_op jit(solution)/shard_map/reshape | solution.py:438
  (1 shorter events, 0.0 us)
Async XLA Ops:
  0.7 0.7 copy-start.3
  1.3 0.7 copy-start.4
  2.0 0.7 copy-start.5
  2.7 0.7 copy-start.6
  3.4 0.7 copy-start.7
  5.6 1.2 %copy-start.2 = (bf16[625,625]{1,0:T(8,128)(2,1)S(1)}, bf16[625,625]{1,0:T(8,128)(2,1)}, u32[]{:S(2)}) copy-start(bf16[625,625]{1,0:T(8,128)(2,1)} %self_ref.1) | copy-start | bytes 2343754
  33.5 1.0 %copy-start = (bf16[3,96,1920]{2,1,0:T(8,128)(2,1)}, bf16[3,96,1920]{2,1,0:T(8,128)(2,1)S(1)}, u32[]{:S(2)}) copy-start(bf16[3,96,1920]{2,1,0:T(8,128)(2,1)S(1)} %get-tuple-element.72.send_ref) | copy-start | bytes 3317764
  34.6 1.2 %copy-start.1 = (bf16[3,96,1920]{2,1,0:T(8,128)(2,1)S(1)}, bf16[3,96,1920]{2,1,0:T(8,128)(2,1)}, u32[]{:S(2)}) copy-start(bf16[3,96,1920]{2,1,0:T(8,128)(2,1)} %copy-done) | copy-start | bytes 3317764

commit v3 on v2

--- a/solution.py
+++ b/solution.py
@@ -11,6 +11,7 @@
 ANY = pl.BlockSpec(memory_space=pl.ANY)
 VMEM = pl.BlockSpec(memory_space=pltpu.VMEM)
 SMEM = pl.BlockSpec(memory_space=pltpu.SMEM)
+HBM = pl.BlockSpec(memory_space=pltpu.HBM)
 CAPACITY = 96
 TABLE = 16
 SCALE, SOURCE_PLACE, SOURCE_COLUMN, TARGET_PLACE, TARGET_COLUMN = 9, 10, 11, 12, 13
@@ -34,7 +35,23 @@
     return lax.shift_right_logical(value, bits), value & (size - 1)
 
 
-def prepare_kernel(places, live_ref, list_ref, target_ref, source_ref, weight_ref, angles_ref, own_ref, rim_ref, table_ref):
+def load(sources, landings, sem):
+    copies = [pltpu.make_async_copy(a, b, sem.at[i]) for i, (a, b) in enumerate(zip(sources, landings))]
+    for copy in copies:
+        copy.start()
+    return copies
+
+
+def prepare_kernel(
+    places, live_ref, list_hbm, target_hbm, source_hbm, weight_hbm, angles_hbm, own_hbm, rim_ref, table_ref,
+    list_ref, target_ref, source_ref, weight_ref, angles_ref, own_ref, sem,
+):
+    for copy in load(
+        [list_hbm, target_hbm, source_hbm, weight_hbm, angles_hbm, own_hbm],
+        [list_ref, target_ref, source_ref, weight_ref, angles_ref, own_ref],
+        sem,
+    ):
+        copy.wait()
     width, grains = own_ref.shape[1:]
     rim, slots = list_ref.shape[1], source_ref.shape[1]
     step = padded(width)
@@ -74,11 +91,11 @@
 
 
 def gather_kernel(
-    sizes, rim_ref, table_ref, own_ref, self_ref, rims_ref, tables_ref, send_ref, mine_ref, most_ref, base_ref,
-    send_sem, recv_sem, own_sem,
+    sizes, rim_ref, table_ref, own_hbm, rims_ref, tables_ref, send_ref, mine_ref, most_ref, own_ref, send_sem, recv_sem, own_sem, load_sem,
 ):
     n_gx, n_gy, n_ha = sizes
     x, y, h = lax.axis_index("gx"), lax.axis_index("gy"), lax.axis_index("ha")
+    loads = load([own_hbm], [own_ref], load_sem)
     near = 1 - 2 * lax.rem(y, 2)
     partner = (x, y + near, h)
     far = lax.rem(y - near + n_gy, n_gy)
@@ -115,8 +132,8 @@
         send(rim_ref, rims_ref.at[(1 - dx) * 3 + 1 + near], beyond[dx + 1], n_ha + 3 + dx) for dx in (-1, 0, 1)
     ]
     rest.append(send(rim_ref, rims_ref.at[4 - near], partner, n_ha))
-    for c in range(3):
-        base_ref[c] = jnp.dot(self_ref[...], own_ref[c], preferred_element_type=F32)
+    for copy in loads:
+        copy.wait()
     for copy in own:
         copy.wait()
     for copy in tables:
@@ -212,11 +229,32 @@
         add_listed(column, rims_ref, own_ref.shape[2], out)
 
 
-def exchange_kernel(n_ha, send_ref, recv_ref, relay_ref, send_sem, recv_sem):
+def finish_kernel(
+    n_ha, opening, round_ref, tables_ref, mine_ref, send_ref, upsample_hbm, normal_hbm, tangent_hbm, *rest
+):
+    if opening:
+        self_hbm, own_hbm, *rest = rest
+    else:
+        before_hbm, *rest = rest
+    out_ref, recv_ref, relay_ref, upsample_ref, normal_ref, tangent_ref, table_ref, rotated_ref, sum_ref, *rest = rest
+    if opening:
+        self_ref, own_ref, *rest = rest
+    else:
+        before_ref, *rest = rest
+    send_sem, recv_sem, load_sem = rest
     x, y, h = lax.axis_index("gx"), lax.axis_index("gy"), lax.axis_index("ha")
     right, left = (x, y, lax.rem(h + 1, n_ha)), (x, y, lax.rem(h + n_ha - 1, n_ha))
-    half = send_ref.shape[1] // 2
+    count = mine_ref.shape[0]
+    nodes, width = upsample_ref.shape
+    grains = out_ref.shape[2]
+    step = padded(width)
+    half = count // 2
     upper, lower = pl.ds(0, half), pl.ds(half, half)
+    loads = load(
+        [upsample_hbm, normal_hbm, tangent_hbm] + ([self_hbm, own_hbm] if opening else [before_hbm]),
+        [upsample_ref, normal_ref, tangent_ref] + ([self_ref, own_ref] if opening else [before_ref]),
+        load_sem,
+    )
     barrier = pltpu.get_barrier_semaphore()
     for device in (right, left):
         pl.semaphore_signal(barrier, inc=1, device_id=device, device_id_type=MESH)
@@ -242,83 +280,87 @@
         send(send_ref.at[0], recv_ref.at[0], right, 2),
         send(send_ref.at[2], recv_ref.at[2], left, 3),
     ]
+
+    first = (round_ref[0] * count).astype(F32)
+    from_place, to_place = table_row(tables_ref, SOURCE_PLACE), table_row(tables_ref, TARGET_PLACE)
+    every = jnp.concatenate([tables_ref[j] for j in range(n_ha)], axis=1)
+    high = every.astype(BF16)
+    middle = (every - high.astype(F32)).astype(BF16)
+    low = (every - high.astype(F32) - middle.astype(F32)).astype(BF16)
+    parts = jnp.concatenate([high, middle, low], axis=0)
+    here = h.astype(F32)
+    for j in range(n_ha):
+        there = lax.rem(h + n_ha - j, n_ha).astype(F32)
+        select = chosen(from_place, to_place, there, here, first, count).astype(BF16)
+        found = lax.dot_general(select, parts, NT, preferred_element_type=F32)
+        table_ref[j * count : (j + 1) * count, :] = (
+            found[:, :TABLE] + found[:, TABLE : 2 * TABLE] + found[:, 2 * TABLE :]
+        )
+
+    def process(blocks, start, end):
+        rows = len(blocks) * count
+        table = jnp.concatenate([table_ref[j * count : (j + 1) * count, :] for j, _ in blocks], axis=0)
+        frame = [table[:, i : i + 1] for i in range(9)]
+        stacked = jnp.concatenate(
+            [ref[:, d * step : d * step + width] for d in range(3) for _, ref in blocks], axis=0
+        )
+
+        def evaluate(begin, size):
+            found = lax.dot_general(stacked, upsample_ref[pl.ds(begin, size), :], NT, preferred_element_type=F32)
+            values = [found[d * rows : (d + 1) * rows].astype(BF16).astype(F32) for d in range(3)]
+            for c in range(3):
+                turned = frame[3 * c] * values[0] + frame[3 * c + 1] * values[1] + frame[3 * c + 2] * values[2]
+                rotated_ref[c * rows : (c + 1) * rows, pl.ds(begin, size)] = turned.astype(BF16)
+
+        tile = 256
+        whole = nodes // tile
+
+        def body(i, carry):
+            evaluate(pl.multiple_of(i * tile, tile), tile)
+            return carry
+
+        lax.fori_loop(0, whole, body, 0)
+        if nodes % tile:
+            evaluate(whole * tile, nodes % tile)
+        normal = jnp.dot(rotated_ref[:rows], normal_ref[...], preferred_element_type=F32)
+        tangent = jnp.dot(rotated_ref[rows : 3 * rows], tangent_ref[...], preferred_element_type=F32)
+        quad = [normal, tangent[:rows], tangent[rows:]]
+        scaling = table[:, SCALE : SCALE + 1]
+        lanes = lax.broadcasted_iota(jnp.int32, (rows, grains), 1).astype(F32)
+        spot = jnp.where(lanes == table[:, TARGET_COLUMN : TARGET_COLUMN + 1], 1.0, 0.0).astype(BF16)
+        spot = jnp.concatenate([spot, spot], axis=0)
+        for c in range(3):
+            given = (frame[c] * quad[0] + frame[3 + c] * quad[1] + frame[6 + c] * quad[2]) * scaling
+            top = given.astype(BF16)
+            rest = (given - top.astype(F32)).astype(BF16)
+            total = lax.dot_general(jnp.concatenate([top, rest], axis=0), spot, TN, preferred_element_type=F32)
+            if not start:
+                total += sum_ref[c]
+            if end:
+                out_ref[c * width : (c + 1) * width, 0, :] = total
+            else:
+                sum_ref[c] = total
+
+    for copy in loads:
+        copy.wait()
+    process([(0, mine_ref)], True, False)
     across[0].wait_recv()
     onward = [send(relay_ref.at[0], recv_ref.at[1, upper], right, 4)]
     across[1].wait_recv()
     onward.append(send(relay_ref.at[1], recv_ref.at[1, lower], left, 5))
-    for copy in across:
+    for copy in direct:
+        copy.wait_recv()
+    process([(1, recv_ref.at[0]), (3, recv_ref.at[2])], False, False)
+    for c in range(3):
+        if opening:
+            sum_ref[c] += jnp.dot(self_ref[...], own_ref[c], preferred_element_type=F32)
+        else:
+            sum_ref[c] += before_ref[c * width : (c + 1) * width, 0, :]
+    for copy in onward:
+        copy.wait_recv()
+    process([(2, recv_ref.at[1])], False, True)
+    for copy in across + direct + onward:
         copy.wait_send()
-    for copy in direct + onward:
-        copy.wait()
-
-
-def apply_kernel(
-    opening, round_ref, place_ref, tables_ref, mine_ref, recv_ref, upsample_ref, normal_ref, tangent_ref,
-    before_ref, out_ref, pick_ref, rotated_ref,
-):
-    places = tables_ref.shape[0]
-    count = mine_ref.shape[0]
-    nodes, width = upsample_ref.shape
-    lines = out_ref.shape[0] // (3 * width)
-    grains = lines * 128
-    step = padded(width)
-    first = (round_ref[0] * count).astype(F32)
-    place = place_ref[0]
-    here = place.astype(F32)
-    pick_ref[:count, :] = mine_ref[...]
-    pick_ref[count:, :] = recv_ref[...]
-    from_place, to_place = table_row(tables_ref, SOURCE_PLACE), table_row(tables_ref, TARGET_PLACE)
-    every = jnp.concatenate([tables_ref[j] for j in range(places)], axis=1)
-    picked_rows = []
-    for j in range(places):
-        there = lax.rem(place + places - j, places).astype(F32)
-        picked_rows.append(chosen(from_place, to_place, there, here, first, count))
-    select = jnp.concatenate(picked_rows, axis=0)
-    table = lax.dot_general(select, every, NT, precision=lax.Precision.HIGHEST, preferred_element_type=F32)
-    frame = [table[:, i : i + 1] for i in range(9)]
-
-    def evaluate(begin, size):
-        values = []
-        for d in range(3):
-            found = lax.dot_general(
-                pick_ref[:, d * step : d * step + width],
-                upsample_ref[pl.ds(begin, size), :],
-                NT,
-                preferred_element_type=F32,
-            )
-            values.append(found.astype(BF16).astype(F32))
-        for c in range(3):
-            turned = frame[3 * c] * values[0] + frame[3 * c + 1] * values[1] + frame[3 * c + 2] * values[2]
-            rotated_ref[c, :, pl.ds(begin, size)] = turned.astype(BF16)
-
-    tile = 256
-    whole = nodes // tile
-
-    def body(i, carry):
-        evaluate(pl.multiple_of(i * tile, tile), tile)
-        return carry
-
-    lax.fori_loop(0, whole, body, 0)
-    if nodes % tile:
-        evaluate(whole * tile, nodes % tile)
-    quad = [
-        jnp.dot(rotated_ref[c], (normal_ref if c == 0 else tangent_ref)[...], preferred_element_type=F32)
-        for c in range(3)
-    ]
-    scaling = table[:, SCALE : SCALE + 1]
-    lanes = lax.broadcasted_iota(jnp.int32, (places * count, grains), 1).astype(F32)
-    spot = jnp.where(lanes == table[:, TARGET_COLUMN : TARGET_COLUMN + 1], 1.0, 0.0).astype(BF16)
-    for c in range(3):
-        given = (frame[c] * quad[0] + frame[3 + c] * quad[1] + frame[6 + c] * quad[2]) * scaling
-        high = given.astype(BF16)
-        low = (given - high.astype(F32)).astype(BF16)
-        total = lax.dot_general(high, spot, TN, preferred_element_type=F32)
-        total += lax.dot_general(low, spot, TN, preferred_element_type=F32)
-        for line in range(lines):
-            spread = pl.ds(c * width * lines + line, width, stride=lines)
-            part = slice(line * 128, (line + 1) * 128)
-            before = before_ref[c, :, part] if opening else before_ref[spread, :]
-            out_ref[spread, :] = total[:, part] + before
 
 
 def shards(
@@ -344,13 +386,21 @@
     count = CAPACITY
     own = density.reshape(3, width, grains)
     normal, tangent = normal_kernel.T, tangent_kernel.T
-    lines = grains // 128
     listed, table = pl.pallas_call(
         functools.partial(prepare_kernel, places),
         out_shape=[jax.ShapeDtypeStruct((rim, span), BF16), jax.ShapeDtypeStruct((TABLE, slots), F32)],
-        in_specs=[SMEM] + [VMEM] * 6,
+        in_specs=[SMEM] + [HBM] * 6,
         out_specs=[VMEM, VMEM],
-        compiler_params=limit(8),
+        scratch_shapes=[
+            pltpu.VMEM((1, rim), jnp.int32),
+            pltpu.VMEM((1, slots), jnp.int32),
+            pltpu.VMEM((1, slots), jnp.int32),
+            pltpu.VMEM((1, slots), F32),
+            pltpu.VMEM((3, 1, slots), F32),
+            pltpu.VMEM((3, width, grains), BF16),
+            pltpu.SemaphoreType.DMA((6,)),
+        ],
+        compiler_params=limit(60),
         name="prepare",
     )(
         live_count.reshape(1),
@@ -361,7 +411,7 @@
         pair_angles.reshape(3, 1, slots),
         own,
     )
-    rims, tables, send, mine, most, base = pl.pallas_call(
+    rims, tables, send, mine, most = pl.pallas_call(
         functools.partial(gather_kernel, sizes),
         out_shape=[
             jax.ShapeDtypeStruct((9, rim, span), BF16),
@@ -369,18 +419,19 @@
             jax.ShapeDtypeStruct((places - 1, count, span), BF16),
             jax.ShapeDtypeStruct((count, span), BF16),
             jax.ShapeDtypeStruct((1, 128), F32),
-            jax.ShapeDtypeStruct((3, width, grains), F32),
         ],
-        in_specs=[ANY, ANY, VMEM, VMEM],
-        out_specs=[VMEM] * 6,
+        in_specs=[ANY, ANY, HBM],
+        out_specs=[VMEM] * 5,
         scratch_shapes=[
+            pltpu.VMEM((3, width, grains), BF16),
             pltpu.SemaphoreType.DMA((places + 7,)),
             pltpu.SemaphoreType.DMA((places + 7,)),
             pltpu.SemaphoreType.DMA((2,)),
+            pltpu.SemaphoreType.DMA((1,)),
         ],
         compiler_params=limit(24, collective_id=0, has_side_effects=True),
         name="gather",
-    )(listed, table, own, self_operator)
+    )(listed, table, own)
     place = lax.axis_index("ha").astype(jnp.int32).reshape(1)
 
     def route(turn):
@@ -396,43 +447,46 @@
             name="route",
         )(turn, place, tables, own, rims)
 
-    def exchange(send):
+    def finish(turn, mine, send, *last):
+        opening = len(last) == 2
+        shape = (3 * width, 1, grains)
         return pl.pallas_call(
-            functools.partial(exchange_kernel, places),
-            out_shape=jax.ShapeDtypeStruct((places - 1, count, span), BF16),
-            in_specs=[ANY],
-            out_specs=ANY,
+            functools.partial(finish_kernel, places, opening),
+            out_shape=jax.ShapeDtypeStruct(shape, F32),
+            in_specs=[SMEM, VMEM, VMEM, ANY] + [HBM] * (3 + len(last)),
+            out_specs=VMEM,
             scratch_shapes=[
+                pltpu.VMEM((places - 1, count, span), BF16),
                 pltpu.VMEM((2, count // 2, span), BF16),
+                pltpu.VMEM((nodes, width), BF16),
+                pltpu.VMEM((nodes, width), BF16),
+                pltpu.VMEM((nodes, width), BF16),
+                pltpu.VMEM((places * count, TABLE), F32),
+                pltpu.VMEM((6 * count, nodes), BF16),
+                pltpu.VMEM((3, width, grains), F32),
+            ]
+            + (
+                [pltpu.VMEM((width, width), BF16), pltpu.VMEM((3, width, grains), BF16)]
+                if opening
+                else [pltpu.VMEM(shape, F32)]
+            )
+            + [
                 pltpu.SemaphoreType.DMA((6,)),
                 pltpu.SemaphoreType.DMA((6,)),
+                pltpu.SemaphoreType.DMA((3 + len(last),)),
             ],
-            compiler_params=limit(4, collective_id=1, has_side_effects=True),
-            name="exchange",
-        )(send).reshape((places - 1) * count, span)
-
-    def apply(turn, mine, received, before, opening):
-        return pl.pallas_call(
-            functools.partial(apply_kernel, opening),
-            out_shape=jax.ShapeDtypeStruct((3 * width * lines, 128), F32),
-            in_specs=[SMEM, SMEM] + [VMEM] * 7,
-            out_specs=VMEM,
-            scratch_shapes=[
-                pltpu.VMEM((places * count, span), BF16),
-                pltpu.VMEM((3, places * count, nodes), BF16),
-            ],
-            compiler_params=limit(40),
-            name="apply",
-        )(turn, place, tables, mine, received, upsample, normal, tangent, before)
+            compiler_params=limit(44, collective_id=1 if opening else 2, has_side_effects=True),
+            name="finish",
+        )(turn, tables, mine, send, upsample, normal, tangent, *last)
 
     turn = jnp.zeros((1,), jnp.int32)
-    result = apply(turn, mine, exchange(send), base, True)
+    result = finish(turn, mine, send, self_operator, own)
     rounds = (most[0, 0].astype(jnp.int32) + count - 1) // count
 
     def again(state):
         now, total = state
         send, mine = route(now.reshape(1))
-        return now + 1, apply(now.reshape(1), mine, exchange(send), total, False)
+        return now + 1, finish(now.reshape(1), mine, send, total)
 
     _, result = lax.while_loop(lambda state: state[0] < rounds, again, (jnp.int32(1), result))
     return result.reshape(3, width, 1, 1, grains)

time: 77.1 us -> 65 us (0.84)
  Pallas kernels: 65.1 us -> 57.9 us
  local copies, waits for them, and re-layouts: 10.8 us -> 5.73 us
    pallas_call x2 -> x1, Pallas kernels: 36.8 us -> 30 us  [finish(): pl.pallas_call(functools.partial(finish_kernel, places, opening), out_sha...]
    reshape x1 -> x0, local copies, waits for them, and re-layouts: 4.04 us -> none  [shards(): return result.reshape(3, width, 1, 1, grains)]
    pallas_call x1, Pallas kernels: 26.7 us -> 25.5 us  [shards(): pl.pallas_call(functools.partial(gather_kernel, sizes), out_shape=[jax.Sh...]
    unnamed x16 -> x9, local copies, waits for them, and re-layouts: 6.74 us -> 5.73 us
    pallas_call x1, Pallas kernels: 1.62 us -> 2.41 us  [shards(): pl.pallas_call(functools.partial(prepare_kernel, places), out_shape=[jax....]
where the time goes in v3:
time: 65 us; the launch traced here: 64.8 us
  Pallas kernels  57.9 us (89%)
  local copies, waits for them, and re-layouts  5.73 us (9%)
  between operations  0.86 us (1%)
    pallas_call x1, Pallas kernels, finish(): pl.pallas_call(functools.partial(finish_kernel, places, opening), out_sha...  30 us
    pallas_call x1, Pallas kernels, shards(): pl.pallas_call(functools.partial(gather_kernel, sizes), out_shape=[jax.Sh...  25.5 us
    unnamed x9, local copies, waits for them, and re-layouts  5.73 us
    pallas_call x1, Pallas kernels, shards(): pl.pallas_call(functools.partial(prepare_kernel, places), out_shape=[jax....  2.41 us

profile of v3, /device:TPU:1, one launch (start us, length us, event | category | flops | bytes accessed | tf_op | source)
XLA Modules:
  0.0 64.8 jit_solution(10963925905196956663)
XLA Ops:
  0.0 0.0 copy-start
  0.7 2.4 %prepare.1 = (bf16[32,1920]{1,0:T(8,128)(2,1)}, f32[16,256]{1,0:T(8,128)}) custom-call(s32[1]{0:T(128)} %bitcast.17.live_ref, s32[1,32]{1,0:T(1,128)} %bitcast.32, s32[1,256]{1,0:T(1,128)} %bitcast.29, s32[1,256]{1,0:T(1,128)} %bitcast.30, f32[1,256]{1,0:T(1,128)} %bitcast.31, f32[3,1,256]{2,1,0:T(1,128)} %bitcast.28, bf16[3,625,256]{2,1,0:T(8,128)(2,1)} %bitcast.24), custom_call_target="tpu_custom_call" | custom-call | tf_op jit(solution)/shard_map/prepare/pallas_call | solution.py:389
  3.1 0.0 copy-start.1
  3.2 0.9 %copy-done.1 = bf16[32,1920]{1,0:T(8,128)(2,1)S(1)} copy-done((bf16[32,1920]{1,0:T(8,128)(2,1)S(1)}, bf16[32,1920]{1,0:T(8,128)(2,1)}, u32[]{:S(2)}) %copy-start.1) | copy-done | bytes 122904
  4.1 0.0 copy-start.2
  4.1 0.7 %copy-done.2 = f32[16,256]{1,0:T(8,128)S(1)} copy-done((f32[16,256]{1,0:T(8,128)S(1)}, f32[16,256]{1,0:T(8,128)}, u32[]{:S(2)}) %copy-start.2) | copy-done | bytes 16408
  4.8 25.5 %gather.1 = (bf16[9,32,1920]{2,1,0:T(8,128)(2,1)}, f32[4,16,256]{2,1,0:T(8,128)S(1)}, bf16[3,96,1920]{2,1,0:T(8,128)(2,1)S(1)}, bf16[96,1920]{1,0:T(8,128)(2,1)S(1)}, f32[1,128]{1,0:T(1,128)S(1)}) custom-call(bf16[32,1920]{1,0:T(8,128)(2,1)S(1)} %copy-done.1, f32[16,256]{1,0:T(8,128)S(1)} %copy-done.2, bf16[3,625,256]{2,1,0:T(8,128)(2,1)} %bitcast.25), custom_call_target="tpu_custom_call" | custom-call | tf_op jit(solution)/shard_map/gather/pallas_call | solution.py:414
  30.4 0.0 copy-done
  30.4 0.0 copy-start.5
  30.4 30.0 %finish.2 = f32[1875,1,256]{2,1,0:T(1,128)} custom-call(s32[1]{0:T(128)} %constant.22.clone.1.round_ref, f32[4,16,256]{2,1,0:T(8,128)S(1)} %get-tuple-element.165.tables_ref, bf16[96,1920]{1,0:T(8,128)(2,1)S(1)} %get-tuple-element.70.mine_ref, bf16[3,96,1920]{2,1,0:T(8,128)(2,1)S(1)} %get-tuple-element.71.send_ref, bf16[2112,625]{1,0:T(8,128)(2,1)} %upsample_hbm.1, ...), custom_call_target="tpu_custom_call" | custom-call | tf_op jit(solution)/shard_map/finish/pallas_call | solution.py:453
  60.4 0.0 copy-done.5
  60.4 0.2 while.10
  60.6 4.1 %copy.22 = f32[3,625,1,1,256]{4,3,2,1,0:T(1,128)} copy(f32[3,625,1,1,256]{4,3,2,1,0:T(1,128)} %bitcast.23) | data formatting | bytes 3840000
Async XLA Ops:
  0.0 30.4 %copy-start = (bf16[625,625]{1,0:T(8,128)(2,1)S(1)}, bf16[625,625]{1,0:T(8,128)(2,1)}, u32[]{:S(2)}) copy-start(bf16[625,625]{1,0:T(8,128)(2,1)} %rest_0_.1) | copy-start | bytes 2343754
  3.1 0.9 %copy-start.1 = (bf16[32,1920]{1,0:T(8,128)(2,1)S(1)}, bf16[32,1920]{1,0:T(8,128)(2,1)}, u32[]{:S(2)}) copy-start(bf16[32,1920]{1,0:T(8,128)(2,1)} %get-tuple-element.67.rim_ref) | copy-start | bytes 368644
  4.1 0.7 %copy-start.2 = (f32[16,256]{1,0:T(8,128)S(1)}, f32[16,256]{1,0:T(8,128)}, u32[]{:S(2)}) copy-start(f32[16,256]{1,0:T(8,128)} %get-tuple-element.68.table_ref) | copy-start | bytes 49156
  30.4 30.0 %copy-start.5 = (bf16[3,625,1,1,256]{4,1,3,2,0:T(8,128)(2,1)S(1)}, bf16[3,625,1,1,256]{4,1,3,2,0:T(8,128)(2,1)}, u32[]{:S(2)}) copy-start(bf16[3,625,1,1,256]{4,1,3,2,0:T(8,128)(2,1)} %param.13) | copy-start | bytes 2880004

commit v4 on v3

--- a/solution.py
+++ b/solution.py
@@ -13,6 +13,7 @@
 SMEM = pl.BlockSpec(memory_space=pltpu.SMEM)
 HBM = pl.BlockSpec(memory_space=pltpu.HBM)
 CAPACITY = 96
+WIDE, NARROW = 1152, 256
 TABLE = 16
 SCALE, SOURCE_PLACE, SOURCE_COLUMN, TARGET_PLACE, TARGET_COLUMN = 9, 10, 11, 12, 13
 NT = (((1,), (1,)), ((), ()))
@@ -91,11 +92,17 @@
 
 
 def gather_kernel(
-    sizes, rim_ref, table_ref, own_hbm, rims_ref, tables_ref, send_ref, mine_ref, most_ref, own_ref, send_sem, recv_sem, own_sem, load_sem,
+    sizes, rim_ref, table_ref, own_hbm, upsample_hbm, normal_hbm, tangent_hbm,
+    rims_ref, tables_ref, send_ref, mine_ref, most_ref, upsample_ref, normal_ref, tangent_ref,
+    own_ref, send_sem, recv_sem, own_sem, load_sem,
 ):
     n_gx, n_gy, n_ha = sizes
     x, y, h = lax.axis_index("gx"), lax.axis_index("gy"), lax.axis_index("ha")
-    loads = load([own_hbm], [own_ref], load_sem)
+    loads = load(
+        [own_hbm, upsample_hbm, normal_hbm, tangent_hbm],
+        [own_ref, upsample_ref, normal_ref, tangent_ref],
+        load_sem,
+    )
     near = 1 - 2 * lax.rem(y, 2)
     partner = (x, y + near, h)
     far = lax.rem(y - near + n_gy, n_gy)
@@ -132,8 +139,7 @@
         send(rim_ref, rims_ref.at[(1 - dx) * 3 + 1 + near], beyond[dx + 1], n_ha + 3 + dx) for dx in (-1, 0, 1)
     ]
     rest.append(send(rim_ref, rims_ref.at[4 - near], partner, n_ha))
-    for copy in loads:
-        copy.wait()
+    loads[0].wait()
     for copy in own:
         copy.wait()
     for copy in tables:
@@ -150,6 +156,8 @@
         )
     for copy in aside:
         copy.wait_send()
+    for copy in loads[1:]:
+        copy.wait()
     for copy in rest:
         copy.wait()
     for column, out in zip(columns, outs):
@@ -229,32 +237,64 @@
         add_listed(column, rims_ref, own_ref.shape[2], out)
 
 
-def finish_kernel(
-    n_ha, opening, round_ref, tables_ref, mine_ref, send_ref, upsample_hbm, normal_hbm, tangent_hbm, *rest
+def add_pairs(table, blocks, upsample_ref, normal_ref, tangent_ref, rotated_ref, grains, tile, pause=None):
+    nodes, width = upsample_ref.shape
+    rows = table.shape[0]
+    step = padded(width)
+    frame = [table[:, i : i + 1] for i in range(9)]
+    stacked = jnp.concatenate([ref[:, d * step : d * step + width] for d in range(3) for ref in blocks], axis=0)
+
+    def evaluate(begin, size):
+        found = lax.dot_general(stacked, upsample_ref[pl.ds(begin, size), :], NT, preferred_element_type=F32)
+        values = [found[d * rows : (d + 1) * rows].astype(BF16).astype(F32) for d in range(3)]
+        for c in range(3):
+            turned = frame[3 * c] * values[0] + frame[3 * c + 1] * values[1] + frame[3 * c + 2] * values[2]
+            rotated_ref[c * rows : (c + 1) * rows, pl.ds(begin, size)] = turned.astype(BF16)
+
+    if tile >= 1024:
+        for begin in range(0, nodes, tile):
+            evaluate(begin, min(tile, nodes - begin))
+    else:
+
+        def body(i, carry):
+            evaluate(pl.multiple_of(i * tile, tile), tile)
+            return carry
+
+        lax.fori_loop(0, nodes // tile, body, 0)
+        if nodes % tile:
+            evaluate(nodes // tile * tile, nodes % tile)
+    if pause is not None:
+        pause()
+    normal = jnp.dot(rotated_ref[:rows], normal_ref[...], preferred_element_type=F32)
+    tangent = jnp.dot(rotated_ref[rows : 3 * rows], tangent_ref[...], preferred_element_type=F32)
+    quad = [normal, tangent[:rows], tangent[rows:]]
+    scaling = table[:, SCALE : SCALE + 1]
+    lanes = lax.broadcasted_iota(jnp.int32, (rows, grains), 1).astype(F32)
+    spot = jnp.where(lanes == table[:, TARGET_COLUMN : TARGET_COLUMN + 1], 1.0, 0.0).astype(BF16)
+    spot = jnp.concatenate([spot, spot], axis=0)
+    totals = []
+    for c in range(3):
+        given = (frame[c] * quad[0] + frame[3 + c] * quad[1] + frame[6 + c] * quad[2]) * scaling
+        top = given.astype(BF16)
+        rest = (given - top.astype(F32)).astype(BF16)
+        totals.append(
+            lax.dot_general(jnp.concatenate([top, rest], axis=0), spot, TN, preferred_element_type=F32)
+        )
+    return totals
+
+
+def exchange_kernel(
+    n_ha, opening, tile, round_ref, tables_ref, mine_ref, send_ref, upsample_ref, normal_ref, tangent_ref, *rest
 ):
     if opening:
-        self_hbm, own_hbm, *rest = rest
-    else:
-        before_hbm, *rest = rest
-    out_ref, recv_ref, relay_ref, upsample_ref, normal_ref, tangent_ref, table_ref, rotated_ref, sum_ref, *rest = rest
-    if opening:
         self_ref, own_ref, *rest = rest
-    else:
-        before_ref, *rest = rest
-    send_sem, recv_sem, load_sem = rest
+    sum_ref, last_ref, table_ref, near_ref, relay_ref, all_ref, rotated_ref, send_sem, recv_sem = rest
     x, y, h = lax.axis_index("gx"), lax.axis_index("gy"), lax.axis_index("ha")
     right, left = (x, y, lax.rem(h + 1, n_ha)), (x, y, lax.rem(h + n_ha - 1, n_ha))
     count = mine_ref.shape[0]
-    nodes, width = upsample_ref.shape
-    grains = out_ref.shape[2]
-    step = padded(width)
+    grains = sum_ref.shape[2]
     half = count // 2
     upper, lower = pl.ds(0, half), pl.ds(half, half)
-    loads = load(
-        [upsample_hbm, normal_hbm, tangent_hbm] + ([self_hbm, own_hbm] if opening else [before_hbm]),
-        [upsample_ref, normal_ref, tangent_ref] + ([self_ref, own_ref] if opening else [before_ref]),
-        load_sem,
-    )
     barrier = pltpu.get_barrier_semaphore()
     for device in (right, left):
         pl.semaphore_signal(barrier, inc=1, device_id=device, device_id_type=MESH)
@@ -272,13 +312,9 @@
         copy.start()
         return copy
 
-    across = [
-        send(send_ref.at[1, upper], relay_ref.at[0], right, 0),
-        send(send_ref.at[1, lower], relay_ref.at[1], left, 1),
-    ]
     direct = [
-        send(send_ref.at[0], recv_ref.at[0], right, 2),
-        send(send_ref.at[2], recv_ref.at[2], left, 3),
+        send(send_ref.at[0], near_ref.at[0], right, 2),
+        send(send_ref.at[2], near_ref.at[1], left, 3),
     ]
 
     first = (round_ref[0] * count).astype(F32)
@@ -289,78 +325,58 @@
     low = (every - high.astype(F32) - middle.astype(F32)).astype(BF16)
     parts = jnp.concatenate([high, middle, low], axis=0)
     here = h.astype(F32)
-    for j in range(n_ha):
+    for place, j in enumerate((0, 1, 3, 2)):
         there = lax.rem(h + n_ha - j, n_ha).astype(F32)
         select = chosen(from_place, to_place, there, here, first, count).astype(BF16)
         found = lax.dot_general(select, parts, NT, preferred_element_type=F32)
-        table_ref[j * count : (j + 1) * count, :] = (
-            found[:, :TABLE] + found[:, TABLE : 2 * TABLE] + found[:, 2 * TABLE :]
-        )
-
-    def process(blocks, start, end):
-        rows = len(blocks) * count
-        table = jnp.concatenate([table_ref[j * count : (j + 1) * count, :] for j, _ in blocks], axis=0)
-        frame = [table[:, i : i + 1] for i in range(9)]
-        stacked = jnp.concatenate(
-            [ref[:, d * step : d * step + width] for d in range(3) for _, ref in blocks], axis=0
-        )
-
-        def evaluate(begin, size):
-            found = lax.dot_general(stacked, upsample_ref[pl.ds(begin, size), :], NT, preferred_element_type=F32)
-            values = [found[d * rows : (d + 1) * rows].astype(BF16).astype(F32) for d in range(3)]
-            for c in range(3):
-                turned = frame[3 * c] * values[0] + frame[3 * c + 1] * values[1] + frame[3 * c + 2] * values[2]
-                rotated_ref[c * rows : (c + 1) * rows, pl.ds(begin, size)] = turned.astype(BF16)
-
-        tile = 256
-        whole = nodes // tile
-
-        def body(i, carry):
-            evaluate(pl.multiple_of(i * tile, tile), tile)
-            return carry
-
-        lax.fori_loop(0, whole, body, 0)
-        if nodes % tile:
-            evaluate(whole * tile, nodes % tile)
-        normal = jnp.dot(rotated_ref[:rows], normal_ref[...], preferred_element_type=F32)
-        tangent = jnp.dot(rotated_ref[rows : 3 * rows], tangent_ref[...], preferred_element_type=F32)
-        quad = [normal, tangent[:rows], tangent[rows:]]
-        scaling = table[:, SCALE : SCALE + 1]
-        lanes = lax.broadcasted_iota(jnp.int32, (rows, grains), 1).astype(F32)
-        spot = jnp.where(lanes == table[:, TARGET_COLUMN : TARGET_COLUMN + 1], 1.0, 0.0).astype(BF16)
-        spot = jnp.concatenate([spot, spot], axis=0)
-        for c in range(3):
-            given = (frame[c] * quad[0] + frame[3 + c] * quad[1] + frame[6 + c] * quad[2]) * scaling
-            top = given.astype(BF16)
-            rest = (given - top.astype(F32)).astype(BF16)
-            total = lax.dot_general(jnp.concatenate([top, rest], axis=0), spot, TN, preferred_element_type=F32)
-            if not start:
-                total += sum_ref[c]
-            if end:
-                out_ref[c * width : (c + 1) * width, 0, :] = total
-            else:
-                sum_ref[c] = total
-
-    for copy in loads:
-        copy.wait()
-    process([(0, mine_ref)], True, False)
-    across[0].wait_recv()
-    onward = [send(relay_ref.at[0], recv_ref.at[1, upper], right, 4)]
-    across[1].wait_recv()
-    onward.append(send(relay_ref.at[1], recv_ref.at[1, lower], left, 5))
+        found = found[:, :TABLE] + found[:, TABLE : 2 * TABLE] + found[:, 2 * TABLE :]
+        if j == 2:
+            table_ref[...] = found
+        else:
+            all_ref[place * count : (place + 1) * count, :] = found
+    weights = (upsample_ref, normal_ref, tangent_ref, rotated_ref, grains, tile)
+    totals = add_pairs(all_ref[:count, :], [mine_ref], *weights)
+    for c in range(3):
+        total = totals[c]
+        if opening:
+            total += jnp.dot(self_ref[...], own_ref[c], preferred_element_type=F32)
+        sum_ref[c] = total
+    for copy in direct:
+        copy.wait_send()
+    across = [
+        send(send_ref.at[1, upper], relay_ref.at[0], right, 0),
+        send(send_ref.at[1, lower], relay_ref.at[1], left, 1),
+    ]
     for copy in direct:
         copy.wait_recv()
-    process([(1, recv_ref.at[0]), (3, recv_ref.at[2])], False, False)
+    onward = []
+
+    def pause():
+        across[0].wait_recv()
+        onward.append(send(relay_ref.at[0], last_ref.at[upper], right, 4))
+        across[1].wait_recv()
+        onward.append(send(relay_ref.at[1], last_ref.at[lower], left, 5))
+
+    totals = add_pairs(all_ref[count:, :], [near_ref.at[0], near_ref.at[1]], *weights, pause)
     for c in range(3):
-        if opening:
-            sum_ref[c] += jnp.dot(self_ref[...], own_ref[c], preferred_element_type=F32)
-        else:
-            sum_ref[c] += before_ref[c * width : (c + 1) * width, 0, :]
+        sum_ref[c] += totals[c]
+    for copy in across:
+        copy.wait_send()
     for copy in onward:
-        copy.wait_recv()
-    process([(2, recv_ref.at[1])], False, True)
-    for copy in across + direct + onward:
-        copy.wait_send()
+        copy.wait()
+
+
+def close_kernel(tile, sum_ref, last_ref, table_ref, upsample_ref, normal_ref, tangent_ref, *rest):
+    *before, out_ref, rotated_ref = rest
+    width, grains = sum_ref.shape[1:]
+    totals = add_pairs(
+        table_ref[...], [last_ref], upsample_ref, normal_ref, tangent_ref, rotated_ref, grains, tile
+    )
+    for c in range(3):
+        total = totals[c] + sum_ref[c]
+        if before:
+            total += before[0][c * width : (c + 1) * width, 0, :]
+        out_ref[c * width : (c + 1) * width, 0, :] = total
 
 
 def shards(
@@ -411,7 +427,7 @@
         pair_angles.reshape(3, 1, slots),
         own,
     )
-    rims, tables, send, mine, most = pl.pallas_call(
+    rims, tables, send, mine, most, *weights = pl.pallas_call(
         functools.partial(gather_kernel, sizes),
         out_shape=[
             jax.ShapeDtypeStruct((9, rim, span), BF16),
@@ -419,19 +435,22 @@
             jax.ShapeDtypeStruct((places - 1, count, span), BF16),
             jax.ShapeDtypeStruct((count, span), BF16),
             jax.ShapeDtypeStruct((1, 128), F32),
+            jax.ShapeDtypeStruct((nodes, width), BF16),
+            jax.ShapeDtypeStruct((nodes, width), BF16),
+            jax.ShapeDtypeStruct((nodes, width), BF16),
         ],
-        in_specs=[ANY, ANY, HBM],
-        out_specs=[VMEM] * 5,
+        in_specs=[ANY, ANY] + [HBM] * 4,
+        out_specs=[VMEM] * 8,
         scratch_shapes=[
             pltpu.VMEM((3, width, grains), BF16),
             pltpu.SemaphoreType.DMA((places + 7,)),
             pltpu.SemaphoreType.DMA((places + 7,)),
             pltpu.SemaphoreType.DMA((2,)),
-            pltpu.SemaphoreType.DMA((1,)),
+            pltpu.SemaphoreType.DMA((4,)),
         ],
         compiler_params=limit(24, collective_id=0, has_side_effects=True),
         name="gather",
-    )(listed, table, own)
+    )(listed, table, own, upsample, normal, tangent)
     place = lax.axis_index("ha").astype(jnp.int32).reshape(1)
 
     def route(turn):
@@ -447,40 +466,45 @@
             name="route",
         )(turn, place, tables, own, rims)
 
-    def finish(turn, mine, send, *last):
-        opening = len(last) == 2
-        shape = (3 * width, 1, grains)
-        return pl.pallas_call(
-            functools.partial(finish_kernel, places, opening),
-            out_shape=jax.ShapeDtypeStruct(shape, F32),
-            in_specs=[SMEM, VMEM, VMEM, ANY] + [HBM] * (3 + len(last)),
-            out_specs=VMEM,
+    def finish(turn, mine, send, before):
+        opening = before is None
+        tile = WIDE if opening else NARROW
+        held = weights if opening else [upsample, normal, tangent]
+        mixed = [self_operator, own] if opening else []
+        total, last, rows = pl.pallas_call(
+            functools.partial(exchange_kernel, places, opening, tile),
+            out_shape=[
+                jax.ShapeDtypeStruct((3, width, grains), F32),
+                jax.ShapeDtypeStruct((count, span), BF16),
+                jax.ShapeDtypeStruct((count, TABLE), F32),
+            ],
+            in_specs=[SMEM, VMEM, VMEM, ANY] + [VMEM] * (3 + len(mixed)),
+            out_specs=[VMEM] * 3,
             scratch_shapes=[
-                pltpu.VMEM((places - 1, count, span), BF16),
+                pltpu.VMEM((2, count, span), BF16),
                 pltpu.VMEM((2, count // 2, span), BF16),
-                pltpu.VMEM((nodes, width), BF16),
-                pltpu.VMEM((nodes, width), BF16),
-                pltpu.VMEM((nodes, width), BF16),
-                pltpu.VMEM((places * count, TABLE), F32),
+                pltpu.VMEM((3 * count, TABLE), F32),
                 pltpu.VMEM((6 * count, nodes), BF16),
-                pltpu.VMEM((3, width, grains), F32),
-            ]
-            + (
-                [pltpu.VMEM((width, width), BF16), pltpu.VMEM((3, width, grains), BF16)]
-                if opening
-                else [pltpu.VMEM(shape, F32)]
-            )
-            + [
                 pltpu.SemaphoreType.DMA((6,)),
                 pltpu.SemaphoreType.DMA((6,)),
-                pltpu.SemaphoreType.DMA((3 + len(last),)),
             ],
-            compiler_params=limit(44, collective_id=1 if opening else 2, has_side_effects=True),
-            name="finish",
-        )(turn, tables, mine, send, upsample, normal, tangent, *last)
+            compiler_params=limit(30, collective_id=1 if opening else 2, has_side_effects=True),
+            name="exchange",
+        )(turn, tables, mine, send, *held, *mixed)
+        ended = [] if opening else [before]
+        return pl.pallas_call(
+            functools.partial(close_kernel, tile),
+            out_shape=jax.ShapeDtypeStruct((3 * width, 1, grains), F32),
+            in_specs=[VMEM] * (6 + len(ended)),
+            out_specs=VMEM,
+            scratch_shapes=[pltpu.VMEM((3 * count, nodes), BF16)],
+            compiler_params=limit(30),
+            name="close",
+        )(total, last, rows, *held, *ended)
 
     turn = jnp.zeros((1,), jnp.int32)
-    result = finish(turn, mine, send, self_operator, own)
+    result = finish(turn, mine, send, None)
+    result, most = lax.optimization_barrier((result, most))
     rounds = (most[0, 0].astype(jnp.int32) + count - 1) // count
 
     def again(state):

time: 65 us -> 55.4 us (0.85)
  Pallas kernels: 57.9 us -> 52.7 us
  local copies, waits for them, and re-layouts: 5.73 us -> 1.63 us
    pallas_call x1 -> x2, Pallas kernels: 30 us -> 24.7 us  [the longest x1 19.7 us: finish(): pl.pallas_call(functools.partial(exchange_kernel, places, opening, tile),...]
    unnamed x9 -> x10, local copies, waits for them, and re-layouts: 5.73 us -> 1.63 us
where the time goes in v4:
time: 55.4 us; the launch traced here: 55.2 us
  Pallas kernels  52.7 us (95%)
  local copies, waits for them, and re-layouts  1.63 us (3%)
  between operations  0.95 us (2%)
    pallas_call x1, Pallas kernels, shards(): pl.pallas_call(functools.partial(gather_kernel, sizes), out_shape=[jax.Sh...  25.6 us
    pallas_call x1, Pallas kernels, finish(): pl.pallas_call(functools.partial(exchange_kernel, places, opening, tile),...  19.7 us
    pallas_call x1, Pallas kernels, finish(): pl.pallas_call(functools.partial(close_kernel, tile), out_shape=jax.Shape...  4.93 us
    pallas_call x1, Pallas kernels, shards(): pl.pallas_call(functools.partial(prepare_kernel, places), out_shape=[jax....  2.41 us
    unnamed x10, local copies, waits for them, and re-layouts  1.63 us

profile of v4, /device:TPU:1, one launch (start us, length us, event | category | flops | bytes accessed | tf_op | source)
XLA Modules:
  0.0 55.2 jit_solution(15251532743585173101)
XLA Ops:
  0.7 2.4 %prepare.1 = (bf16[32,1920]{1,0:T(8,128)(2,1)}, f32[16,256]{1,0:T(8,128)}) custom-call(s32[1]{0:T(128)} %bitcast.17.live_ref, s32[1,32]{1,0:T(1,128)} %bitcast.31, s32[1,256]{1,0:T(1,128)} %bitcast.28, s32[1,256]{1,0:T(1,128)} %bitcast.29, f32[1,256]{1,0:T(1,128)} %bitcast.30, f32[3,1,256]{2,1,0:T(1,128)} %bitcast.27, bf16[3,625,256]{2,1,0:T(8,128)(2,1)} %bitcast.23), custom_call_target="tpu_custom_call" | custom-call | tf_op jit(solution)/shard_map/prepare/pallas_call | solution.py:405
  3.1 0.0 copy-start.1
  3.1 0.9 %copy-done.1 = bf16[32,1920]{1,0:T(8,128)(2,1)S(1)} copy-done((bf16[32,1920]{1,0:T(8,128)(2,1)S(1)}, bf16[32,1920]{1,0:T(8,128)(2,1)}, u32[]{:S(2)}) %copy-start.1) | copy-done | bytes 122904
  4.0 0.0 copy-start.2
  4.0 0.7 %copy-done.2 = f32[16,256]{1,0:T(8,128)S(1)} copy-done((f32[16,256]{1,0:T(8,128)S(1)}, f32[16,256]{1,0:T(8,128)}, u32[]{:S(2)}) %copy-start.2) | copy-done | bytes 16408
  4.7 0.0 copy-start
  4.7 0.0 copy-start.7
  4.7 25.6 %gather.1 = (bf16[9,32,1920]{2,1,0:T(8,128)(2,1)}, f32[4,16,256]{2,1,0:T(8,128)S(1)}, bf16[3,96,1920]{2,1,0:T(8,128)(2,1)S(1)}, bf16[96,1920]{1,0:T(8,128)(2,1)S...) custom-call(bf16[32,1920]{1,0:T(8,128)(2,1)S(1)} %copy-done.1, ...), custom_call_target="tpu_custom_call" | custom-call | tf_op jit(solution)/shard_map/gather/pallas_call | solution.py:430
  30.3 0.0 copy-done
  30.3 0.0 copy-done.7
  30.3 19.7 %exchange.2 = (f32[3,625,256]{2,1,0:T(8,128)S(1)}, bf16[96,1920]{1,0:T(8,128)(2,1)S(1)}, f32[96,16]{1,0:T(8,128)S(1)}) custom-call(s32[1]{0:T(128)} %constant.22.clone.1.round_ref, f32[4,16,256]{2,1,0:T(8,128)S(1)} %get-tuple-element.190.tables_ref, bf16[96,1920]{1,0:T(8,128)(2,1)S(1)} %get-tuple-element.81.mine_ref, ...), custom_call_target="tpu_custom_call" | custom-call | tf_op jit(solution)/shard_map/exchange/pallas_call | solution.py:474
  50.0 0.0 copy-start.3
  50.1 4.9 %close.2 = f32[1875,1,256]{2,1,0:T(1,128)} custom-call(f32[3,625,256]{2,1,0:T(8,128)S(1)} %get-tuple-element.86.sum_ref, bf16[96,1920]{1,0:T(8,128)(2,1)S(1)} %get-tuple-element.87.last_ref, f32[96,16]{1,0:T(8,128)S(1)} %get-tuple-element.88.table_ref, bf16[2112,625]{1,0:T(8,128)(2,1)S(1)} %get-tuple-element.83.upsample_ref, ...), custom_call_target="tpu_custom_call" | custom-call | tf_op jit(solution)/shard_map/close/pallas_call | solution.py:495
  55.1 0.0 copy-done.3
  (1 shorter events, 0.0 us)
Async XLA Ops:
  3.1 0.9 %copy-start.1 = (bf16[32,1920]{1,0:T(8,128)(2,1)S(1)}, bf16[32,1920]{1,0:T(8,128)(2,1)}, u32[]{:S(2)}) copy-start(bf16[32,1920]{1,0:T(8,128)(2,1)} %get-tuple-element.78.rim_ref) | copy-start | bytes 368644
  4.0 0.7 %copy-start.2 = (f32[16,256]{1,0:T(8,128)S(1)}, f32[16,256]{1,0:T(8,128)}, u32[]{:S(2)}) copy-start(f32[16,256]{1,0:T(8,128)} %get-tuple-element.79.table_ref) | copy-start | bytes 49156
  4.7 25.6 %copy-start = (bf16[625,625]{1,0:T(8,128)(2,1)S(1)}, bf16[625,625]{1,0:T(8,128)(2,1)}, u32[]{:S(2)}) copy-start(bf16[625,625]{1,0:T(8,128)(2,1)} %rest_0_.1) | copy-start | bytes 2343754
  4.7 25.6 %copy-start.7 = (bf16[3,625,1,1,256]{4,1,3,2,0:T(8,128)(2,1)S(1)}, bf16[3,625,1,1,256]{4,1,3,2,0:T(8,128)(2,1)}, u32[]{:S(2)}) copy-start(bf16[3,625,1,1,256]{4,1,3,2,0:T(8,128)(2,1)} %param.13) | copy-start | bytes 2880004
  50.0 5.0 %copy-start.3 = (bf16[2112,625]{1,0:T(8,128)(2,1)S(1)}, bf16[2112,625]{1,0:T(8,128)(2,1)}, u32[]{:S(2)}) copy-start(bf16[2112,625]{1,0:T(8,128)(2,1)} %upsample_hbm.1) | copy-start | bytes 7920004

commit v5 on v4

--- a/solution.py
+++ b/solution.py
@@ -12,7 +12,7 @@
 VMEM = pl.BlockSpec(memory_space=pltpu.VMEM)
 SMEM = pl.BlockSpec(memory_space=pltpu.SMEM)
 HBM = pl.BlockSpec(memory_space=pltpu.HBM)
-CAPACITY = 96
+CAPACITY = 88
 WIDE, NARROW = 1152, 256
 TABLE = 16
 SCALE, SOURCE_PLACE, SOURCE_COLUMN, TARGET_PLACE, TARGET_COLUMN = 9, 10, 11, 12, 13
@@ -109,8 +109,10 @@
     barrier = pltpu.get_barrier_semaphore()
     mates = [(x, y, lax.rem(h + j, n_ha)) for j in range(1, n_ha)]
     sides = [(lax.rem(x + dx + n_gx, n_gx), y, h) for dx in (-1, 1)]
-    beyond = [(lax.rem(x + dx + n_gx, n_gx), far, h) for dx in (-1, 0, 1)]
-    peers = mates + sides + beyond + [partner]
+    beyond = [(lax.rem(x + dx + n_gx, n_gx), far, h) for dx in (-1, 1)]
+    ahead = (x, far, h)
+    relays = lax.rem(x, 2) == lax.rem(y, 2)
+    peers = mates + sides + beyond + [ahead, partner]
     for device in peers:
         pl.semaphore_signal(barrier, inc=1, device_id=device, device_id_type=MESH)
     own = [
@@ -121,47 +123,72 @@
         copy.start()
     pl.semaphore_wait(barrier, len(peers))
 
-    def send(source, landing, device, slot):
-        copy = pltpu.make_async_remote_copy(
+    def send(source, landing, device, leaving, arriving):
+        return pltpu.make_async_remote_copy(
             src_ref=source,
             dst_ref=landing,
-            send_sem=send_sem.at[slot],
-            recv_sem=recv_sem.at[slot],
+            send_sem=send_sem.at[leaving],
+            recv_sem=recv_sem.at[arriving],
             device_id=device,
             device_id_type=MESH,
         )
+
+    tables = [send(table_ref, tables_ref.at[h], mates[j], j, j) for j in range(n_ha - 1)]
+    for copy in tables:
         copy.start()
-        return copy
-
-    tables = [send(table_ref, tables_ref.at[h], mates[j], j) for j in range(n_ha - 1)]
-    aside = [send(rim_ref, rims_ref.at[(1 - dx) * 3 + 1], sides[(dx + 1) // 2], n_ha + dx) for dx in (-1, 1)]
-    rest = [
-        send(rim_ref, rims_ref.at[(1 - dx) * 3 + 1 + near], beyond[dx + 1], n_ha + 3 + dx) for dx in (-1, 0, 1)
+    aside, middle, onward, wide, across = [], [], [], [], []
+    for i, dx in enumerate((-1, 1)):
+        column, away = (dx + 1) * 3 + 1, (1 - dx) * 3 + 1
+        aside.append(send(rim_ref, rims_ref.at[away], sides[i], n_ha + i, n_ha + 1 - i))
+        onward.append(send(rims_ref.at[column], rims_ref.at[column - near], partner, n_ha + 2 + i, n_ha + 2 + i))
+        across.append(send(rims_ref.at[column], rims_ref.at[column + near], ahead, n_ha + 4 + i, n_ha + 8 + i))
+        wide.append(send(rim_ref, rims_ref.at[away + near], beyond[i], n_ha + 6 + i, n_ha + 9 - i))
+    middle = [
+        send(rim_ref, rims_ref.at[4 - near], partner, n_ha + 8, n_ha + 4),
+        send(rim_ref, rims_ref.at[4 + near], ahead, n_ha + 9, n_ha + 5),
     ]
-    rest.append(send(rim_ref, rims_ref.at[4 - near], partner, n_ha))
+    for copy in aside + middle:
+        copy.start()
+
+    @pl.when(relays)
+    def _():
+        for copy in wide:
+            copy.start()
+
     loads[0].wait()
     for copy in own:
         copy.wait()
     for copy in tables:
         copy.wait()
-    columns = route_columns(jnp.float32(0.0), h, tables_ref, mine_ref.shape[0])
+    column = route_columns(jnp.float32(0.0), h, tables_ref, mine_ref.shape[0])
     outs = [mine_ref] + [send_ref.at[j] for j in range(n_ha - 1)]
-    for column, out in zip(columns, outs):
-        pick_own(column, own_ref, out)
+    pick_own(column, own_ref, outs)
     most_ref[...] = jnp.broadcast_to(longest(tables_ref), most_ref.shape)
-    for i, dx in enumerate((-1, 1)):
-        aside[i].wait_recv()
-        rest.append(
-            send(rims_ref.at[(1 - dx) * 3 + 1], rims_ref.at[(1 - dx) * 3 + 1 - near], partner, n_ha + 5 + i)
-        )
+    for copy in aside:
+        copy.wait_recv()
+    for copy in onward:
+        copy.start()
+
+    @pl.when(relays)
+    def _():
+        for copy in across:
+            copy.start()
+
+    for copy in loads[1:]:
+        copy.wait()
     for copy in aside:
         copy.wait_send()
-    for copy in loads[1:]:
+    for copy in middle + onward:
         copy.wait()
-    for copy in rest:
-        copy.wait()
-    for column, out in zip(columns, outs):
-        add_listed(column, rims_ref, own_ref.shape[2], out)
+    for copy in across:
+        copy.wait_recv()
+
+    @pl.when(relays)
+    def _():
+        for copy in wide + across:
+            copy.wait_send()
+
+    add_listed(column, rims_ref, own_ref.shape[2], outs)
 
 
 def ranks(mask):
@@ -195,7 +222,7 @@
         there = lax.rem(place + j, places).astype(F32)
         select = chosen(from_place, to_place, here, there, first, count)
         columns.append(jnp.sum(select * column_row, axis=1, keepdims=True) - 1.0)
-    return columns
+    return jnp.concatenate(columns, axis=0)
 
 
 def longest(tables_ref):
@@ -209,32 +236,38 @@
     return most
 
 
-def pick_own(column, own_ref, out):
-    count, (width, grains) = column.shape[0], own_ref.shape[1:]
-    step = padded(width)
-    lanes = lax.broadcasted_iota(jnp.int32, (count, grains), 1).astype(F32)
+def pick_own(column, own_ref, outs):
+    rows, (width, grains) = column.shape[0], own_ref.shape[1:]
+    step, count = padded(width), outs[0].shape[0]
+    lanes = lax.broadcasted_iota(jnp.int32, (rows, grains), 1).astype(F32)
     pick = jnp.where(lanes == column, 1.0, 0.0).astype(BF16)
-    out[...] = jnp.zeros(out.shape, BF16)
+    for out in outs:
+        out[...] = jnp.zeros(out.shape, BF16)
     for c in range(3):
         found = lax.dot_general(pick, own_ref[c], NT, preferred_element_type=F32)
-        out[:, c * step : c * step + width] = found.astype(BF16)
-
-
-def add_listed(column, rims_ref, grains, out):
-    count, groups, rim = column.shape[0], rims_ref.shape[0], rims_ref.shape[1]
-    lanes = lax.broadcasted_iota(jnp.int32, (count, groups * rim), 1).astype(F32) + float(grains)
+        for j, out in enumerate(outs):
+            out[:, c * step : c * step + width] = found[j * count : (j + 1) * count].astype(BF16)
+
+
+def add_listed(column, rims_ref, grains, outs):
+    rows, groups, rim = column.shape[0], rims_ref.shape[0], rims_ref.shape[1]
+    span, count = rims_ref.shape[2], outs[0].shape[0]
+    lanes = lax.broadcasted_iota(jnp.int32, (rows, groups * rim), 1).astype(F32) + float(grains)
     pick = jnp.where(lanes == column, 1.0, 0.0).astype(BF16)
-    rims = rims_ref[...].reshape(groups * rim, rims_ref.shape[2])
-    found = jnp.dot(pick, rims, preferred_element_type=F32)
-    out[...] = (out[...].astype(F32) + found).astype(BF16)
+    for begin in range(0, span, span // 3):
+        part = slice(begin, begin + span // 3)
+        rims = rims_ref[:, :, part].reshape(groups * rim, span // 3)
+        found = jnp.dot(pick, rims, preferred_element_type=F32)
+        for j, out in enumerate(outs):
+            out[:, part] = (out[:, part].astype(F32) + found[j * count : (j + 1) * count]).astype(BF16)
 
 
 def route_kernel(round_ref, place_ref, tables_ref, own_ref, rims_ref, send_ref, mine_ref):
     count = mine_ref.shape[0]
-    columns = route_columns((round_ref[0] * count).astype(F32), place_ref[0], tables_ref, count)
-    for column, out in zip(columns, [mine_ref] + [send_ref.at[j] for j in range(send_ref.shape[0])]):
-        pick_own(column, own_ref, out)
-        add_listed(column, rims_ref, own_ref.shape[2], out)
+    column = route_columns((round_ref[0] * count).astype(F32), place_ref[0], tables_ref, count)
+    outs = [mine_ref] + [send_ref.at[j] for j in range(send_ref.shape[0])]
+    pick_own(column, own_ref, outs)
+    add_listed(column, rims_ref, own_ref.shape[2], outs)
 
 
 def add_pairs(table, blocks, upsample_ref, normal_ref, tangent_ref, rotated_ref, grains, tile, pause=None):
@@ -293,8 +326,9 @@
     right, left = (x, y, lax.rem(h + 1, n_ha)), (x, y, lax.rem(h + n_ha - 1, n_ha))
     count = mine_ref.shape[0]
     grains = sum_ref.shape[2]
-    half = count // 2
-    upper, lower = pl.ds(0, half), pl.ds(half, half)
+    half = relay_ref.shape[1]
+    upper, lower = pl.ds(0, half), pl.ds(half, count - half)
+    lesser = pl.ds(0, count - half)
     barrier = pltpu.get_barrier_semaphore()
     for device in (right, left):
         pl.semaphore_signal(barrier, inc=1, device_id=device, device_id_type=MESH)
@@ -345,7 +379,7 @@
         copy.wait_send()
     across = [
         send(send_ref.at[1, upper], relay_ref.at[0], right, 0),
-        send(send_ref.at[1, lower], relay_ref.at[1], left, 1),
+        send(send_ref.at[1, lower], relay_ref.at[1, lesser], left, 1),
     ]
     for copy in direct:
         copy.wait_recv()
@@ -355,7 +389,7 @@
         across[0].wait_recv()
         onward.append(send(relay_ref.at[0], last_ref.at[upper], right, 4))
         across[1].wait_recv()
-        onward.append(send(relay_ref.at[1], last_ref.at[lower], left, 5))
+        onward.append(send(relay_ref.at[1, lesser], last_ref.at[lower], left, 5))
 
     totals = add_pairs(all_ref[count:, :], [near_ref.at[0], near_ref.at[1]], *weights, pause)
     for c in range(3):
@@ -443,8 +477,8 @@
         out_specs=[VMEM] * 8,
         scratch_shapes=[
             pltpu.VMEM((3, width, grains), BF16),
-            pltpu.SemaphoreType.DMA((places + 7,)),
-            pltpu.SemaphoreType.DMA((places + 7,)),
+            pltpu.SemaphoreType.DMA((places + 10,)),
+            pltpu.SemaphoreType.DMA((places + 10,)),
             pltpu.SemaphoreType.DMA((2,)),
             pltpu.SemaphoreType.DMA((4,)),
         ],
@@ -482,7 +516,7 @@
             out_specs=[VMEM] * 3,
             scratch_shapes=[
                 pltpu.VMEM((2, count, span), BF16),
-                pltpu.VMEM((2, count // 2, span), BF16),
+                pltpu.VMEM((2, (count // 2 + 15) // 16 * 16, span), BF16),
                 pltpu.VMEM((3 * count, TABLE), F32),
                 pltpu.VMEM((6 * count, nodes), BF16),
                 pltpu.SemaphoreType.DMA((6,)),

time: 55.4 us -> 53 us (0.957)
  Pallas kernels: 52.7 us -> 50.2 us
    pallas_call x1, Pallas kernels: 19.7 us -> 18.1 us  [finish(): pl.pallas_call(functools.partial(exchange_kernel, places, opening, tile),...]
    pallas_call x1, Pallas kernels: 25.6 us -> 24.9 us  [shards(): pl.pallas_call(functools.partial(gather_kernel, sizes), out_shape=[jax.Sh...]
where the time goes in v5:
time: 53 us; the launch traced here: 52.8 us
  Pallas kernels  50.2 us (95%)
  local copies, waits for them, and re-layouts  1.63 us (3%)
  between operations  0.95 us (2%)
    pallas_call x1, Pallas kernels, shards(): pl.pallas_call(functools.partial(gather_kernel, sizes), out_shape=[jax.Sh...  24.9 us
    pallas_call x1, Pallas kernels, finish(): pl.pallas_call(functools.partial(exchange_kernel, places, opening, tile),...  18.1 us
    pallas_call x1, Pallas kernels, finish(): pl.pallas_call(functools.partial(close_kernel, tile), out_shape=jax.Shape...  4.86 us
    pallas_call x1, Pallas kernels, shards(): pl.pallas_call(functools.partial(prepare_kernel, places), out_shape=[jax....  2.41 us
    unnamed x10, local copies, waits for them, and re-layouts  1.63 us

profile of v5, /device:TPU:1, one launch (start us, length us, event | category | flops | bytes accessed | tf_op | source)
XLA Modules:
  0.0 52.8 jit_solution(6072142168300297459)
XLA Ops:
  0.7 2.4 %prepare.1 = (bf16[32,1920]{1,0:T(8,128)(2,1)}, f32[16,256]{1,0:T(8,128)}) custom-call(s32[1]{0:T(128)} %bitcast.17.live_ref, s32[1,32]{1,0:T(1,128)} %bitcast.31, s32[1,256]{1,0:T(1,128)} %bitcast.28, s32[1,256]{1,0:T(1,128)} %bitcast.29, f32[1,256]{1,0:T(1,128)} %bitcast.30, f32[3,1,256]{2,1,0:T(1,128)} %bitcast.27, bf16[3,625,256]{2,1,0:T(8,128)(2,1)} %bitcast.23), custom_call_target="tpu_custom_call" | custom-call | tf_op jit(solution)/shard_map/prepare/pallas_call | solution.py:439
  3.1 0.0 copy-start.1
  3.1 0.9 %copy-done.1 = bf16[32,1920]{1,0:T(8,128)(2,1)S(1)} copy-done((bf16[32,1920]{1,0:T(8,128)(2,1)S(1)}, bf16[32,1920]{1,0:T(8,128)(2,1)}, u32[]{:S(2)}) %copy-start.1) | copy-done | bytes 122904
  4.0 0.0 copy-start.2
  4.0 0.7 %copy-done.2 = f32[16,256]{1,0:T(8,128)S(1)} copy-done((f32[16,256]{1,0:T(8,128)S(1)}, f32[16,256]{1,0:T(8,128)}, u32[]{:S(2)}) %copy-start.2) | copy-done | bytes 16408
  4.7 0.0 copy-start
  4.7 0.0 copy-start.7
  4.7 24.9 %gather.1 = (bf16[9,32,1920]{2,1,0:T(8,128)(2,1)}, f32[4,16,256]{2,1,0:T(8,128)S(1)}, bf16[3,88,1920]{2,1,0:T(8,128)(2,1)S(1)}, bf16[88,1920]{1,0:T(8,128)(2,1)S...) custom-call(bf16[32,1920]{1,0:T(8,128)(2,1)S(1)} %copy-done.1, ...), custom_call_target="tpu_custom_call" | custom-call | tf_op jit(solution)/shard_map/gather/pallas_call | solution.py:464
  29.6 0.0 copy-done
  29.6 0.0 copy-done.7
  29.6 18.1 %exchange.2 = (f32[3,625,256]{2,1,0:T(8,128)S(1)}, bf16[88,1920]{1,0:T(8,128)(2,1)S(1)}, f32[88,16]{1,0:T(8,128)S(1)}) custom-call(s32[1]{0:T(128)} %constant.22.clone.1.round_ref, f32[4,16,256]{2,1,0:T(8,128)S(1)} %get-tuple-element.190.tables_ref, bf16[88,1920]{1,0:T(8,128)(2,1)S(1)} %get-tuple-element.81.mine_ref, ...), custom_call_target="tpu_custom_call" | custom-call | tf_op jit(solution)/shard_map/exchange/pallas_call | solution.py:508
  47.7 0.0 copy-start.3
  47.7 4.9 %close.2 = f32[1875,1,256]{2,1,0:T(1,128)} custom-call(f32[3,625,256]{2,1,0:T(8,128)S(1)} %get-tuple-element.86.sum_ref, bf16[88,1920]{1,0:T(8,128)(2,1)S(1)} %get-tuple-element.87.last_ref, f32[88,16]{1,0:T(8,128)S(1)} %get-tuple-element.88.table_ref, bf16[2112,625]{1,0:T(8,128)(2,1)S(1)} %get-tuple-element.83.upsample_ref, ...), custom_call_target="tpu_custom_call" | custom-call | tf_op jit(solution)/shard_map/close/pallas_call | solution.py:529
  52.6 0.0 copy-done.3
  (1 shorter events, 0.0 us)
Async XLA Ops:
  3.1 0.9 %copy-start.1 = (bf16[32,1920]{1,0:T(8,128)(2,1)S(1)}, bf16[32,1920]{1,0:T(8,128)(2,1)}, u32[]{:S(2)}) copy-start(bf16[32,1920]{1,0:T(8,128)(2,1)} %get-tuple-element.78.rim_ref) | copy-start | bytes 368644
  4.0 0.7 %copy-start.2 = (f32[16,256]{1,0:T(8,128)S(1)}, f32[16,256]{1,0:T(8,128)}, u32[]{:S(2)}) copy-start(f32[16,256]{1,0:T(8,128)} %get-tuple-element.79.table_ref) | copy-start | bytes 49156
  4.7 24.9 %copy-start = (bf16[625,625]{1,0:T(8,128)(2,1)S(1)}, bf16[625,625]{1,0:T(8,128)(2,1)}, u32[]{:S(2)}) copy-start(bf16[625,625]{1,0:T(8,128)(2,1)} %rest_0_.1) | copy-start | bytes 2343754
  4.7 24.9 %copy-start.7 = (bf16[3,625,1,1,256]{4,1,3,2,0:T(8,128)(2,1)S(1)}, bf16[3,625,1,1,256]{4,1,3,2,0:T(8,128)(2,1)}, u32[]{:S(2)}) copy-start(bf16[3,625,1,1,256]{4,1,3,2,0:T(8,128)(2,1)} %param.13) | copy-start | bytes 2880004
  47.7 4.9 %copy-start.3 = (bf16[2112,625]{1,0:T(8,128)(2,1)S(1)}, bf16[2112,625]{1,0:T(8,128)(2,1)}, u32[]{:S(2)}) copy-start(bf16[2112,625]{1,0:T(8,128)(2,1)} %upsample_hbm.1) | copy-start | bytes 7920004

commit v6 on v5

--- a/solution.py
+++ b/solution.py
@@ -44,29 +44,24 @@
 
 
 def prepare_kernel(
-    places, live_ref, list_hbm, target_hbm, source_hbm, weight_hbm, angles_hbm, own_hbm, rim_ref, table_ref,
+    places, live_ref, list_hbm, target_hbm, source_hbm, weight_hbm, angles_hbm, own_hbm, packed_ref,
     list_ref, target_ref, source_ref, weight_ref, angles_ref, own_ref, sem,
 ):
-    for copy in load(
+    loads = load(
         [list_hbm, target_hbm, source_hbm, weight_hbm, angles_hbm, own_hbm],
         [list_ref, target_ref, source_ref, weight_ref, angles_ref, own_ref],
         sem,
-    ):
-        copy.wait()
+    )
+    packed_ref[...] = jnp.zeros_like(packed_ref)
     width, grains = own_ref.shape[1:]
     rim, slots = list_ref.shape[1], source_ref.shape[1]
     step = padded(width)
-    square = [lax.broadcasted_iota(jnp.int32, (rim, rim), axis) for axis in (0, 1)]
-    listed = jnp.where(square[0] == square[1], list_ref[...].astype(F32), 0.0)
-    listed = jnp.sum(listed, axis=1, keepdims=True)
-    lanes = lax.broadcasted_iota(jnp.int32, (rim, grains), 1).astype(F32)
-    pick = jnp.where(listed == lanes, 1.0, 0.0).astype(BF16)
-    rim_ref[...] = jnp.zeros_like(rim_ref)
-    for c in range(3):
-        found = lax.dot_general(pick, own_ref[c], NT, preferred_element_type=F32)
-        rim_ref[:, c * step : c * step + width] = found.astype(BF16)
-    c0, c1, c2 = (jnp.cos(angles_ref[i]) for i in range(3))
-    s0, s1, s2 = (jnp.sin(angles_ref[i]) for i in range(3))
+    for copy in loads[:5]:
+        copy.wait()
+    angles = jnp.concatenate([angles_ref[i] for i in range(3)], axis=0)
+    cosines, sines = jnp.cos(angles), jnp.sin(angles)
+    c0, c1, c2 = (cosines[i : i + 1] for i in range(3))
+    s0, s1, s2 = (sines[i : i + 1] for i in range(3))
     frame = [
         c0 * c1 * c2 - s0 * s2, -(c0 * c1 * s2) - s0 * c2, c0 * s1,
         s0 * c1 * c2 + c0 * s2, -(s0 * c1 * s2) + c0 * c2, s0 * s1,
@@ -86,17 +81,32 @@
         jnp.where(alive, target_place, -1).astype(F32),
         target_column.astype(F32),
     ]
-    table_ref[...] = jnp.zeros_like(table_ref)
-    for i, row in enumerate(rows):
-        table_ref[i : i + 1, :] = row
+    rows += [jnp.zeros((1, slots), F32)] * (TABLE - len(rows))
+    table = jnp.concatenate(rows, axis=0)
+    high = table.astype(BF16)
+    middle = (table - high.astype(F32)).astype(BF16)
+    low = (table - high.astype(F32) - middle.astype(F32)).astype(BF16)
+    for i, part in enumerate((high, middle, low)):
+        packed_ref[rim : rim + TABLE, i * slots : (i + 1) * slots] = part
+    square = [lax.broadcasted_iota(jnp.int32, (rim, rim), axis) for axis in (0, 1)]
+    listed = jnp.where(square[0] == square[1], list_ref[...].astype(F32), 0.0)
+    listed = jnp.sum(listed, axis=1, keepdims=True)
+    lanes = lax.broadcasted_iota(jnp.int32, (rim, grains), 1).astype(F32)
+    pick = jnp.where(listed == lanes, 1.0, 0.0).astype(BF16)
+    loads[5].wait()
+    for c in range(3):
+        found = lax.dot_general(pick, own_ref[c], NT, preferred_element_type=F32)
+        packed_ref[:rim, c * step : c * step + width] = found.astype(BF16)
 
 
 def gather_kernel(
-    sizes, rim_ref, table_ref, own_hbm, upsample_hbm, normal_hbm, tangent_hbm,
+    sizes, packed_ref, own_hbm, upsample_hbm, normal_hbm, tangent_hbm,
     rims_ref, tables_ref, send_ref, mine_ref, most_ref, upsample_ref, normal_ref, tangent_ref,
     own_ref, send_sem, recv_sem, own_sem, load_sem,
 ):
     n_gx, n_gy, n_ha = sizes
+    rim_ref = packed_ref.at[pl.ds(0, rims_ref.shape[1])]
+    table_ref = packed_ref.at[pl.ds(rims_ref.shape[1], TABLE), pl.ds(0, tables_ref.shape[2])]
     x, y, h = lax.axis_index("gx"), lax.axis_index("gy"), lax.axis_index("ha")
     loads = load(
         [own_hbm, upsample_hbm, normal_hbm, tangent_hbm],
@@ -201,8 +211,18 @@
     return total - mask
 
 
-def table_row(tables_ref, row):
-    return jnp.concatenate([tables_ref[j, row : row + 1, :] for j in range(tables_ref.shape[0])], axis=1)
+def table_parts(tables_ref):
+    places, slots = tables_ref.shape[0], tables_ref.shape[2] // 3
+    return [
+        jnp.concatenate([tables_ref[j, :, i * slots : (i + 1) * slots] for j in range(places)], axis=1)
+        for i in range(3)
+    ]
+
+
+def table_places(tables_ref):
+    high, middle, _ = (part.astype(F32) for part in table_parts(tables_ref))
+    whole = high + middle
+    return [whole[i : i + 1] for i in (SOURCE_PLACE, TARGET_PLACE, SOURCE_COLUMN)]
 
 
 def chosen(from_place, to_place, source, target, first, count):
@@ -215,8 +235,8 @@
 def route_columns(first, place, tables_ref, count):
     places = tables_ref.shape[0]
     here = place.astype(F32)
-    from_place, to_place = table_row(tables_ref, SOURCE_PLACE), table_row(tables_ref, TARGET_PLACE)
-    column_row = table_row(tables_ref, SOURCE_COLUMN) + 1.0
+    from_place, to_place, column_row = table_places(tables_ref)
+    column_row = column_row + 1.0
     columns = []
     for j in range(places):
         there = lax.rem(place + j, places).astype(F32)
@@ -227,7 +247,7 @@
 
 def longest(tables_ref):
     places = tables_ref.shape[0]
-    from_place, to_place = table_row(tables_ref, SOURCE_PLACE), table_row(tables_ref, TARGET_PLACE)
+    from_place, to_place, _ = table_places(tables_ref)
     most = jnp.zeros((1, 1), F32)
     for source in range(places):
         for target in range(places):
@@ -352,12 +372,8 @@
     ]
 
     first = (round_ref[0] * count).astype(F32)
-    from_place, to_place = table_row(tables_ref, SOURCE_PLACE), table_row(tables_ref, TARGET_PLACE)
-    every = jnp.concatenate([tables_ref[j] for j in range(n_ha)], axis=1)
-    high = every.astype(BF16)
-    middle = (every - high.astype(F32)).astype(BF16)
-    low = (every - high.astype(F32) - middle.astype(F32)).astype(BF16)
-    parts = jnp.concatenate([high, middle, low], axis=0)
+    from_place, to_place, _ = table_places(tables_ref)
+    parts = jnp.concatenate(table_parts(tables_ref), axis=0)
     here = h.astype(F32)
     for place, j in enumerate((0, 1, 3, 2)):
         there = lax.rem(h + n_ha - j, n_ha).astype(F32)
@@ -436,11 +452,11 @@
     count = CAPACITY
     own = density.reshape(3, width, grains)
     normal, tangent = normal_kernel.T, tangent_kernel.T
-    listed, table = pl.pallas_call(
+    packed = pl.pallas_call(
         functools.partial(prepare_kernel, places),
-        out_shape=[jax.ShapeDtypeStruct((rim, span), BF16), jax.ShapeDtypeStruct((TABLE, slots), F32)],
+        out_shape=jax.ShapeDtypeStruct((rim + TABLE, span), BF16),
         in_specs=[SMEM] + [HBM] * 6,
-        out_specs=[VMEM, VMEM],
+        out_specs=VMEM,
         scratch_shapes=[
             pltpu.VMEM((1, rim), jnp.int32),
             pltpu.VMEM((1, slots), jnp.int32),
@@ -465,7 +481,7 @@
         functools.partial(gather_kernel, sizes),
         out_shape=[
             jax.ShapeDtypeStruct((9, rim, span), BF16),
-            jax.ShapeDtypeStruct((places, TABLE, slots), F32),
+            jax.ShapeDtypeStruct((places, TABLE, 3 * slots), BF16),
             jax.ShapeDtypeStruct((places - 1, count, span), BF16),
             jax.ShapeDtypeStruct((count, span), BF16),
             jax.ShapeDtypeStruct((1, 128), F32),
@@ -473,7 +489,7 @@
             jax.ShapeDtypeStruct((nodes, width), BF16),
             jax.ShapeDtypeStruct((nodes, width), BF16),
         ],
-        in_specs=[ANY, ANY] + [HBM] * 4,
+        in_specs=[ANY] + [HBM] * 4,
         out_specs=[VMEM] * 8,
         scratch_shapes=[
             pltpu.VMEM((3, width, grains), BF16),
@@ -484,7 +500,7 @@
         ],
         compiler_params=limit(24, collective_id=0, has_side_effects=True),
         name="gather",
-    )(listed, table, own, upsample, normal, tangent)
+    )(packed, own, upsample, normal, tangent)
     place = lax.axis_index("ha").astype(jnp.int32).reshape(1)
 
     def route(turn):

time: 53 us -> 52.3 us (0.987)
  local copies, waits for them, and re-layouts: 1.63 us -> 0.93 us
    unnamed x10 -> x8, local copies, waits for them, and re-layouts: 1.63 us -> 0.93 us
where the time goes in v6:
time: 52.3 us; the launch traced here: 52.1 us
  Pallas kernels  50.2 us (96%)
  between operations  0.95 us (2%)
  local copies, waits for them, and re-layouts  0.93 us (2%)
    pallas_call x1, Pallas kernels, shards(): pl.pallas_call(functools.partial(gather_kernel, sizes), out_shape=[jax.Sh...  24.8 us
    pallas_call x1, Pallas kernels, finish(): pl.pallas_call(functools.partial(exchange_kernel, places, opening, tile),...  18.1 us
    pallas_call x1, Pallas kernels, finish(): pl.pallas_call(functools.partial(close_kernel, tile), out_shape=jax.Shape...  4.86 us
    pallas_call x1, Pallas kernels, shards(): pl.pallas_call(functools.partial(prepare_kernel, places), out_shape=jax.S...  2.42 us

profile of v6, /device:TPU:1, one launch (start us, length us, event | category | flops | bytes accessed | tf_op | source)
XLA Modules:
  0.0 52.1 jit_solution(6531613928084880189)
XLA Ops:
  0.7 2.4 %prepare.1.packed_ref = bf16[48,1920]{1,0:T(8,128)(2,1)} custom-call(s32[1]{0:T(128)} %bitcast.17.live_ref, s32[1,32]{1,0:T(1,128)} %bitcast.31, s32[1,256]{1,0:T(1,128)} %bitcast.28, s32[1,256]{1,0:T(1,128)} %bitcast.29, f32[1,256]{1,0:T(1,128)} %bitcast.30, f32[3,1,256]{2,1,0:T(1,128)} %bitcast.27, bf16[3,625,256]{2,1,0:T(8,128)(2,1)} %bitcast.23), custom_call_target="tpu_custom_call" | custom-call | tf_op jit(solution)/shard_map/prepare/pallas_call | solution.py:455
  3.1 0.0 copy-start.1
  3.1 0.9 %copy-done.1 = bf16[48,1920]{1,0:T(8,128)(2,1)S(1)} copy-done((bf16[48,1920]{1,0:T(8,128)(2,1)S(1)}, bf16[48,1920]{1,0:T(8,128)(2,1)}, u32[]{:S(2)}) %copy-start.1) | copy-done | bytes 184344
  4.0 0.0 copy-start
  4.0 0.0 copy-start.6
  4.0 24.8 %gather.1 = (bf16[9,32,1920]{2,1,0:T(8,128)(2,1)}, bf16[4,16,768]{2,1,0:T(8,128)(2,1)S(1)}, bf16[3,88,1920]{2,1,0:T(8,128)(2,1)S(1)}, bf16[88,1920]{1,0:T(8,128)...) custom-call(bf16[48,1920]{1,0:T(8,128)(2,1)S(1)} %copy-done.1, ...), custom_call_target="tpu_custom_call" | custom-call | tf_op jit(solution)/shard_map/gather/pallas_call | solution.py:480
  28.9 0.0 copy-done
  28.9 0.0 copy-done.6
  28.9 18.1 %exchange.2 = (f32[3,625,256]{2,1,0:T(8,128)S(1)}, bf16[88,1920]{1,0:T(8,128)(2,1)S(1)}, f32[88,16]{1,0:T(8,128)S(1)}) custom-call(s32[1]{0:T(128)} %constant.22.clone.1.round_ref, bf16[4,16,768]{2,1,0:T(8,128)(2,1)S(1)} %get-tuple-element.186.tables_ref, bf16[88,1920]{1,0:T(8,128)(2,1)S(1)} %get-tuple-element.77.mine_ref, ...), custom_call_target="tpu_custom_call" | custom-call | tf_op jit(solution)/shard_map/exchange/pallas_call | solution.py:524
  47.0 0.0 copy-start.2
  47.0 4.9 %close.2 = f32[1875,1,256]{2,1,0:T(1,128)} custom-call(f32[3,625,256]{2,1,0:T(8,128)S(1)} %get-tuple-element.82.sum_ref, bf16[88,1920]{1,0:T(8,128)(2,1)S(1)} %get-tuple-element.83.last_ref, f32[88,16]{1,0:T(8,128)S(1)} %get-tuple-element.84.table_ref, bf16[2112,625]{1,0:T(8,128)(2,1)S(1)} %get-tuple-element.79.upsample_ref, ...), custom_call_target="tpu_custom_call" | custom-call | tf_op jit(solution)/shard_map/close/pallas_call | solution.py:545
  51.9 0.0 copy-done.2
  (1 shorter events, 0.0 us)
Async XLA Ops:
  3.1 0.9 %copy-start.1 = (bf16[48,1920]{1,0:T(8,128)(2,1)S(1)}, bf16[48,1920]{1,0:T(8,128)(2,1)}, u32[]{:S(2)}) copy-start(bf16[48,1920]{1,0:T(8,128)(2,1)} %prepare.1.packed_ref) | copy-start | bytes 552964
  4.0 24.9 %copy-start = (bf16[625,625]{1,0:T(8,128)(2,1)S(1)}, bf16[625,625]{1,0:T(8,128)(2,1)}, u32[]{:S(2)}) copy-start(bf16[625,625]{1,0:T(8,128)(2,1)} %rest_0_.1) | copy-start | bytes 2343754
  4.0 24.9 %copy-start.6 = (bf16[3,625,1,1,256]{4,1,3,2,0:T(8,128)(2,1)S(1)}, bf16[3,625,1,1,256]{4,1,3,2,0:T(8,128)(2,1)}, u32[]{:S(2)}) copy-start(bf16[3,625,1,1,256]{4,1,3,2,0:T(8,128)(2,1)} %param.13) | copy-start | bytes 2880004
  47.0 4.9 %copy-start.2 = (bf16[2112,625]{1,0:T(8,128)(2,1)S(1)}, bf16[2112,625]{1,0:T(8,128)(2,1)}, u32[]{:S(2)}) copy-start(bf16[2112,625]{1,0:T(8,128)(2,1)} %upsample_hbm.1) | copy-start | bytes 7920004

commit v7 on v6

--- a/solution.py
+++ b/solution.py
@@ -307,6 +307,8 @@
     if tile >= 1024:
         for begin in range(0, nodes, tile):
             evaluate(begin, min(tile, nodes - begin))
+            if pause is not None:
+                pause()
     else:
 
         def body(i, carry):
@@ -316,8 +318,6 @@
         lax.fori_loop(0, nodes // tile, body, 0)
         if nodes % tile:
             evaluate(nodes // tile * tile, nodes % tile)
-    if pause is not None:
-        pause()
     normal = jnp.dot(rotated_ref[:rows], normal_ref[...], preferred_element_type=F32)
     tangent = jnp.dot(rotated_ref[rows : 3 * rows], tangent_ref[...], preferred_element_type=F32)
     quad = [normal, tangent[:rows], tangent[rows:]]
@@ -346,9 +346,8 @@
     right, left = (x, y, lax.rem(h + 1, n_ha)), (x, y, lax.rem(h + n_ha - 1, n_ha))
     count = mine_ref.shape[0]
     grains = sum_ref.shape[2]
-    half = relay_ref.shape[1]
-    upper, lower = pl.ds(0, half), pl.ds(half, count - half)
-    lesser = pl.ds(0, count - half)
+    size = relay_ref.shape[1]
+    sizes = [size, size, size, count - 3 * size]
     barrier = pltpu.get_barrier_semaphore()
     for device in (right, left):
         pl.semaphore_signal(barrier, inc=1, device_id=device, device_id_type=MESH)
@@ -367,8 +366,13 @@
         return copy
 
     direct = [
-        send(send_ref.at[0], near_ref.at[0], right, 2),
-        send(send_ref.at[2], near_ref.at[1], left, 3),
+        send(send_ref.at[0], near_ref.at[0], right, 0),
+        send(send_ref.at[2], near_ref.at[1], left, 1),
+    ]
+    pieces = [(0, right), (2, left), (1, right), (3, left)]
+    across = [
+        send(send_ref.at[1, pl.ds(i * size, sizes[i])], relay_ref.at[i, pl.ds(0, sizes[i])], device, 2 + i)
+        for i, device in pieces
     ]
 
     first = (round_ref[0] * count).astype(F32)
@@ -392,25 +396,22 @@
             total += jnp.dot(self_ref[...], own_ref[c], preferred_element_type=F32)
         sum_ref[c] = total
     for copy in direct:
-        copy.wait_send()
-    across = [
-        send(send_ref.at[1, upper], relay_ref.at[0], right, 0),
-        send(send_ref.at[1, lower], relay_ref.at[1, lesser], left, 1),
-    ]
-    for copy in direct:
         copy.wait_recv()
     onward = []
 
     def pause():
-        across[0].wait_recv()
-        onward.append(send(relay_ref.at[0], last_ref.at[upper], right, 4))
-        across[1].wait_recv()
-        onward.append(send(relay_ref.at[1, lesser], last_ref.at[lower], left, 5))
+        for copy, (i, device) in list(zip(across, pieces))[len(onward) : len(onward) + 2]:
+            copy.wait_recv()
+            onward.append(
+                send(relay_ref.at[i, pl.ds(0, sizes[i])], last_ref.at[pl.ds(i * size, sizes[i])], device, 6 + i)
+            )
 
     totals = add_pairs(all_ref[count:, :], [near_ref.at[0], near_ref.at[1]], *weights, pause)
     for c in range(3):
         sum_ref[c] += totals[c]
-    for copy in across:
+    while len(onward) < len(pieces):
+        pause()
+    for copy in direct + across:
         copy.wait_send()
     for copy in onward:
         copy.wait()
@@ -532,11 +533,11 @@
             out_specs=[VMEM] * 3,
             scratch_shapes=[
                 pltpu.VMEM((2, count, span), BF16),
-                pltpu.VMEM((2, (count // 2 + 15) // 16 * 16, span), BF16),
+                pltpu.VMEM((4, (count // 4 + 7) // 8 * 8, span), BF16),
                 pltpu.VMEM((3 * count, TABLE), F32),
                 pltpu.VMEM((6 * count, nodes), BF16),
-                pltpu.SemaphoreType.DMA((6,)),
-                pltpu.SemaphoreType.DMA((6,)),
+                pltpu.SemaphoreType.DMA((10,)),
+                pltpu.SemaphoreType.DMA((10,)),
             ],
             compiler_params=limit(30, collective_id=1 if opening else 2, has_side_effects=True),
             name="exchange",

time: 52.3 us -> 51.8 us (level)
  no operation moved by 1% of the time
where the time goes in v7:
time: 51.8 us; the launch traced here: 51.7 us
  Pallas kernels  49.8 us (96%)
  between operations  0.95 us (2%)
  local copies, waits for them, and re-layouts  0.93 us (2%)
    pallas_call x1, Pallas kernels, shards(): pl.pallas_call(functools.partial(gather_kernel, sizes), out_shape=[jax.Sh...  24.8 us
    pallas_call x1, Pallas kernels, finish(): pl.pallas_call(functools.partial(exchange_kernel, places, opening, tile),...  17.7 us
    pallas_call x1, Pallas kernels, finish(): pl.pallas_call(functools.partial(close_kernel, tile), out_shape=jax.Shape...  4.84 us
    pallas_call x1, Pallas kernels, shards(): pl.pallas_call(functools.partial(prepare_kernel, places), out_shape=jax.S...  2.42 us

profile of v7, /device:TPU:1, one launch (start us, length us, event | category | flops | bytes accessed | tf_op | source)
XLA Modules:
  0.0 51.7 jit_solution(7446547194934805463)
XLA Ops:
  0.7 2.4 %prepare.1.packed_ref = bf16[48,1920]{1,0:T(8,128)(2,1)} custom-call(s32[1]{0:T(128)} %bitcast.17.live_ref, s32[1,32]{1,0:T(1,128)} %bitcast.31, s32[1,256]{1,0:T(1,128)} %bitcast.28, s32[1,256]{1,0:T(1,128)} %bitcast.29, f32[1,256]{1,0:T(1,128)} %bitcast.30, f32[3,1,256]{2,1,0:T(1,128)} %bitcast.27, bf16[3,625,256]{2,1,0:T(8,128)(2,1)} %bitcast.23), custom_call_target="tpu_custom_call" | custom-call | tf_op jit(solution)/shard_map/prepare/pallas_call | solution.py:456
  3.1 0.0 copy-start.1
  3.1 0.9 %copy-done.1 = bf16[48,1920]{1,0:T(8,128)(2,1)S(1)} copy-done((bf16[48,1920]{1,0:T(8,128)(2,1)S(1)}, bf16[48,1920]{1,0:T(8,128)(2,1)}, u32[]{:S(2)}) %copy-start.1) | copy-done | bytes 184344
  4.0 0.0 copy-start
  4.0 0.0 copy-start.6
  4.0 24.8 %gather.1 = (bf16[9,32,1920]{2,1,0:T(8,128)(2,1)}, bf16[4,16,768]{2,1,0:T(8,128)(2,1)S(1)}, bf16[3,88,1920]{2,1,0:T(8,128)(2,1)S(1)}, bf16[88,1920]{1,0:T(8,128)...) custom-call(bf16[48,1920]{1,0:T(8,128)(2,1)S(1)} %copy-done.1, ...), custom_call_target="tpu_custom_call" | custom-call | tf_op jit(solution)/shard_map/gather/pallas_call | solution.py:481
  28.9 0.0 copy-done
  28.9 0.0 copy-done.6
  28.9 17.7 %exchange.2 = (f32[3,625,256]{2,1,0:T(8,128)S(1)}, bf16[88,1920]{1,0:T(8,128)(2,1)S(1)}, f32[88,16]{1,0:T(8,128)S(1)}) custom-call(s32[1]{0:T(128)} %constant.22.clone.1.round_ref, bf16[4,16,768]{2,1,0:T(8,128)(2,1)S(1)} %get-tuple-element.186.tables_ref, bf16[88,1920]{1,0:T(8,128)(2,1)S(1)} %get-tuple-element.77.mine_ref, ...), custom_call_target="tpu_custom_call" | custom-call | tf_op jit(solution)/shard_map/exchange/pallas_call | solution.py:525
  46.6 0.0 copy-start.2
  46.6 4.8 %close.2 = f32[1875,1,256]{2,1,0:T(1,128)} custom-call(f32[3,625,256]{2,1,0:T(8,128)S(1)} %get-tuple-element.82.sum_ref, bf16[88,1920]{1,0:T(8,128)(2,1)S(1)} %get-tuple-element.83.last_ref, f32[88,16]{1,0:T(8,128)S(1)} %get-tuple-element.84.table_ref, bf16[2112,625]{1,0:T(8,128)(2,1)S(1)} %get-tuple-element.79.upsample_ref, ...), custom_call_target="tpu_custom_call" | custom-call | tf_op jit(solution)/shard_map/close/pallas_call | solution.py:546
  51.5 0.0 copy-done.2
  (1 shorter events, 0.0 us)
Async XLA Ops:
  3.1 0.9 %copy-start.1 = (bf16[48,1920]{1,0:T(8,128)(2,1)S(1)}, bf16[48,1920]{1,0:T(8,128)(2,1)}, u32[]{:S(2)}) copy-start(bf16[48,1920]{1,0:T(8,128)(2,1)} %prepare.1.packed_ref) | copy-start | bytes 552964
  4.0 24.9 %copy-start = (bf16[625,625]{1,0:T(8,128)(2,1)S(1)}, bf16[625,625]{1,0:T(8,128)(2,1)}, u32[]{:S(2)}) copy-start(bf16[625,625]{1,0:T(8,128)(2,1)} %rest_0_.1) | copy-start | bytes 2343754
  4.0 24.9 %copy-start.6 = (bf16[3,625,1,1,256]{4,1,3,2,0:T(8,128)(2,1)S(1)}, bf16[3,625,1,1,256]{4,1,3,2,0:T(8,128)(2,1)}, u32[]{:S(2)}) copy-start(bf16[3,625,1,1,256]{4,1,3,2,0:T(8,128)(2,1)} %param.13) | copy-start | bytes 2880004
  46.6 4.9 %copy-start.2 = (bf16[2112,625]{1,0:T(8,128)(2,1)S(1)}, bf16[2112,625]{1,0:T(8,128)(2,1)}, u32[]{:S(2)}) copy-start(bf16[2112,625]{1,0:T(8,128)(2,1)} %upsample_hbm.1) | copy-start | bytes 7920004
